TPU v7x, 32 devices: a 4x2x2 block of a 4x4x8 slice. The times are simulated.
32 devices in a mesh: dp: 4 (over y, z), tp: 8 (over x, core).
Axes of the slice: x: 4, y: 2, z: 2, core: 2. Of those that a mesh axis runs over, the one named last changes fastest.
The devices are a block of a 4x4x8 slice.
Arguments:
- x_norm: bfloat16 [16384, 896], P(('dp', 'tp')), parts along dimension 0
- grad_y: bfloat16 [16384, 896], P(('dp', 'tp')), parts along dimension 0
- u_gate: bfloat16 [16384, 4864], P('dp', 'tp'), parts along dimension 0
- u_up: bfloat16 [16384, 4864], P('dp', 'tp'), parts along dimension 0
- w_gate: bfloat16 [896, 4864], P(None, 'tp')
- w_up: bfloat16 [896, 4864], P(None, 'tp')
- w_down: bfloat16 [4864, 896], P('tp')
- x_in: bfloat16 [16384, 896], P(('dp', 'tp')), parts along dimension 0
- gamma: bfloat16 [896], replicated
- grad_res: bfloat16 [16384, 896], P(('dp', 'tp')), parts along dimension 0
- attn_out: bfloat16 [16384, 896], P('dp', 'tp'), parts along dimension 0
- w_out: bfloat16 [896, 896], P('tp')
Outputs:
- output 1: bfloat16 [16384, 896], P(('dp', 'tp')), parts along dimension 0
- output 2: bfloat16 [16384, 896], P('dp', 'tp'), parts along dimension 0
- output 3: float32 [3584, 4864], P('dp', 'tp'), parts along dimension 0
- output 4: float32 [3584, 4864], P('dp', 'tp'), parts along dimension 0
- output 5: float32 [19456, 896], P(('dp', 'tp')), parts along dimension 0
- output 6: float32 [3584, 896], P(('dp', 'tp')), parts along dimension 0
There are 4 independent parts. A program takes and returns all parts, laid end to end along the dimension named above; an argument that names none is the same for every part.
All inputs are finite; a program needn't handle non-finite values.
Results may differ from a plain program's by a relative error of at most 0.0148603.
Values are sent between devices in bfloat16 or wider.
A program may use at most 768 MiB of HBM per device.

v0:
```python
import jax
import jax.numpy as jnp
from jax import lax
from jax.sharding import PartitionSpec as P

NORM_EPS = 1e-5
CONTRACT_ROWS = (((0,), (0,)), ((), ()))
CONTRACT_COLS = (((1,), (1,)), ((), ()))


def rms_backward(grad_x, x_in, gamma, grad_res):
    xin_f = x_in.astype(jnp.float32)
    inv_rms = lax.rsqrt(jnp.mean(xin_f * xin_f, axis=-1, keepdims=True) + NORM_EPS)
    scaled = grad_x.astype(jnp.float32) * gamma.astype(jnp.float32)
    proj_mean = jnp.mean(scaled * xin_f, axis=-1, keepdims=True)
    return (grad_res.astype(jnp.float32)
            + inv_rms * (scaled - xin_f * (inv_rms * inv_rms) * proj_mean)).astype(jnp.bfloat16)


def solution(mesh):
    token_spec = P(("dp", "tp"), None)
    split_cols = P("dp", "tp")
    weight_cols = P(None, "tp")
    weight_rows = P("tp", None)

    def local_backward(x_norm, grad_y, u_gate, u_up, w_gate, w_up, w_down, x_in, gamma, grad_res, attn_out, w_out):
        x_full = lax.all_gather(x_norm, "tp", axis=0, tiled=True)
        gy_full = lax.all_gather(grad_y, "tp", axis=0, tiled=True)
        gate_f = u_gate.astype(jnp.float32)
        up_f = u_up.astype(jnp.float32)
        sig_gate = jax.nn.sigmoid(gate_f)
        act_gate = gate_f * sig_gate
        silu_grad = sig_gate * (1.0 + gate_f * (1.0 - sig_gate))
        hidden_z = (act_gate * up_f).astype(jnp.bfloat16)
        gw_down = lax.dot_general(hidden_z, gy_full, CONTRACT_ROWS, preferred_element_type=jnp.float32)
        grad_h = lax.dot_general(gy_full, w_down, CONTRACT_COLS, preferred_element_type=jnp.float32)
        grad_up = (grad_h * act_gate).astype(jnp.bfloat16)
        grad_gate = (grad_h * up_f * silu_grad).astype(jnp.bfloat16)
        part_x = (lax.dot_general(grad_gate, w_gate, CONTRACT_COLS, preferred_element_type=jnp.float32)
                  + lax.dot_general(grad_up, w_up, CONTRACT_COLS, preferred_element_type=jnp.float32))
        grad_x = lax.psum_scatter(part_x.astype(jnp.bfloat16), "tp", scatter_dimension=0, tiled=True)
        gw_gate = lax.dot_general(x_full, grad_gate, CONTRACT_ROWS, preferred_element_type=jnp.float32)
        gw_up = lax.dot_general(x_full, grad_up, CONTRACT_ROWS, preferred_element_type=jnp.float32)
        grad_sum = rms_backward(grad_x, x_in, gamma, grad_res)
        gs_full = lax.all_gather(grad_sum, "tp", axis=0, tiled=True)
        grad_attn = lax.dot_general(gs_full, w_out, CONTRACT_COLS, preferred_element_type=jnp.float32).astype(jnp.bfloat16)
        gw_out = lax.dot_general(attn_out, gs_full, CONTRACT_ROWS, preferred_element_type=jnp.float32)
        return grad_sum, grad_attn, gw_gate, gw_up, gw_down, gw_out

    return jax.shard_map(
        local_backward,
        mesh=mesh,
        in_specs=(token_spec, token_spec, split_cols, split_cols, weight_cols, weight_cols, weight_rows,
                  token_spec, P(None), token_spec, split_cols, weight_rows),
        out_specs=(token_spec, split_cols, split_cols, split_cols, token_spec, token_spec),
        check_vma=False,
    )
```

profile of v0, /device:TPU:81, one launch (start us, length us, event | category | flops | bytes accessed | tf_op | source)
XLA Modules:
  0.0 237.9 jit_solution(6484965608473911482)
XLA Ops:
  7.2 0.0 copy-start
  7.2 0.1 all-gather.4.cloned.1.call-start
  7.3 0.7 all-gather.4.cloned.1.call-update
  8.0 0.0 copy-start.9
  8.0 0.1 reduce-scatter.2.cloned.1.call-start
  8.1 48.1 %all-gather.4.cloned.1.call-done = bf16[4096,896]{1,0:T(8,128)(2,1)} async-done(((bf16[512,896]{1,0:T(8,128)(2,1)}), bf16[4096,896]{1,0:T(8,128)(2,1)}) %all-gather.4.cloned.1.call-update) | async-done | bytes 7340048 | tf_op jit(solution)/shard_map/all_gather | solution.py:28
  56.2 0.0 copy-done
  56.2 14.6 %multiply_convert_fusion = (bf16[4096,608]{0,1:T(8,128)(2,1)}, bf16[4096,608]{0,1:T(8,128)(2,1)}) fusion(bf16[4096,608]{0,1:T(8,128)(2,1)} %param.14, bf16[4096,608]{0,1:T(8,128)(2,1)} %param.15, bf16[4096,896]{1,0:T(8,128)(2,1)} %all-gather.4.cloned.1.call-done, bf16[608,896]{1,0:T(8,128)(2,1)S(1)} %copy-done), kind=kOutput, calls=%fused_computation.14 | convolution fusion | flops 4500094976 | bytes 28352512 | tf_op jit(solution)/shard_map/dot_general | solution.py:36
  70.8 0.0 copy-done.9
  70.8 8.6 %fusion.19 = f32[4096,896]{1,0:T(8,128)S(1)} fusion(bf16[4096,608]{0,1:T(8,128)(2,1)} %get-tuple-element.9, bf16[896,608]{0,1:T(8,128)(2,1)S(1)} %copy-done.9), kind=kOutput, calls=%fused_computation.35 | convolution fusion | flops 4462739456 | bytes 20750336 | tf_op jit(solution)/shard_map/dot_general | solution.py:39
  79.3 0.0 copy-done.10
  79.4 11.1 %add_convert_fusion = bf16[4096,896]{1,0:T(8,128)(2,1)} fusion(f32[4096,896]{1,0:T(8,128)S(1)} %fusion.19, bf16[4096,608]{0,1:T(8,128)(2,1)} %get-tuple-element.8, bf16[896,608]{0,1:T(8,128)(2,1)S(1)} %copy-done.10), kind=kOutput, calls=%fused_computation.3 | convolution fusion | flops 4470079488 | bytes 28090368 | tf_op jit(solution)/shard_map/dot_general | solution.py:40
  90.5 0.1 reduce-scatter.2.cloned.1.call-update
  90.6 0.1 all-gather.8.cloned.1.call-start
  90.6 0.7 all-gather.8.cloned.1.call-update
  91.4 0.2 all-gather.6.cloned.1.call-start
  91.6 0.0 copy-done.7
  91.6 42.8 %reduce-scatter.2.cloned.1.call-done = bf16[512,896]{1,0:T(8,128)(2,1)} async-done(((bf16[4096,896]{1,0:T(8,128)(2,1)}), bf16[512,896]{1,0:T(8,128)(2,1)}) %reduce-scatter.2.cloned.1.call-update) | async-done | bytes 917520 | tf_op jit(solution)/shard_map/reduce_scatter | solution.py:41
  134.4 0.0 copy-done.3
  134.5 1.7 fusion.10
  136.2 2.8 %fusion.15 = bf16[512,896]{1,0:T(8,128)(2,1)} fusion(bf16[512,896]{1,0:T(8,128)(2,1)S(1)} %copy-done.3, bf16[512,896]{1,0:T(8,128)(2,1)} %reduce-scatter.2.cloned.1.call-done, bf16[512,896]{1,0:T(8,128)(2,1)S(1)} %copy-done.5, f32[512]{0:T(512)S(1)} %broadcast_multiply_fusion, f32[512]{0:T(512)S(1)} %get-tuple-element.11, f32[896]{0:T(1024)S(1)} %convert_element_type.44, ...), kind=kLoop, calls=%fused_computation.25 | loop fusion | flops 4587520 | bytes 3679744 | tf_op jit(solution)/shard_map/convert_element_type | solution.py:17
  139.0 0.1 all-gather.6.cloned.1.call-update
  139.0 39.6 %all-gather.8.cloned.1.call-done = bf16[4096,896]{1,0:T(8,128)(2,1)} async-done(((bf16[512,896]{1,0:T(8,128)(2,1)}), bf16[4096,896]{1,0:T(8,128)(2,1)}) %all-gather.8.cloned.1.call-update) | async-done | bytes 7340048 | tf_op jit(solution)/shard_map/all_gather | solution.py:27
  178.6 10.4 %convolution_bitcast_fusion = f32[896,608]{0,1:T(8,128)} fusion(bf16[4096,608]{0,1:T(8,128)(2,1)} %get-tuple-element.8, bf16[4096,896]{1,0:T(8,128)(2,1)} %all-gather.8.cloned.1.call-done), kind=kOutput, calls=%fused_computation.28 | convolution fusion | flops 4462739456 | bytes 14499840 | tf_op jit(solution)/shard_map/dot_general | solution.py:43
  189.0 0.0 slice-start.5
  189.0 8.3 %convolution_bitcast_fusion.1 = f32[896,608]{0,1:T(8,128)} fusion(bf16[4096,608]{0,1:T(8,128)(2,1)} %get-tuple-element.9, bf16[4096,896]{1,0:T(8,128)(2,1)S(1)} %copy-done.8), kind=kOutput, calls=%fused_computation.29 | convolution fusion | flops 4462739456 | bytes 14499840 | tf_op jit(solution)/shard_map/dot_general | solution.py:42
  197.4 0.0 copy-start.4
  197.4 7.2 %fusion.8 = f32[608,896]{1,0:T(8,128)} fusion(bf16[4096,896]{1,0:T(8,128)(2,1)S(1)} %bitcast.22, bf16[4096,608]{0,1:T(8,128)(2,1)S(1)} %bitcast.26, bf16[4096,608]{0,1:T(8,128)(2,1)S(1)} %bitcast.24), kind=kOutput, calls=%fused_computation.15 | convolution fusion | flops 4482662400 | bytes 19480576 | tf_op jit(solution)/shard_map/dot_general | solution.py:35
  204.6 18.1 %all-gather.6.cloned.1.call-done = bf16[4096,896]{1,0:T(8,128)(2,1)} async-done(((bf16[512,896]{1,0:T(8,128)(2,1)}), bf16[4096,896]{1,0:T(8,128)(2,1)}) %all-gather.6.cloned.1.call-update) | async-done | bytes 7340048 | tf_op jit(solution)/shard_map/all_gather | solution.py:45
  222.8 0.0 copy-done.4
  222.8 5.3 %convolution_bitcast_fusion.2 = f32[112,896]{1,0:T(8,128)} fusion(bf16[4096,112]{0,1:T(8,128)(2,1)S(1)} %copy-done.4, bf16[4096,896]{1,0:T(8,128)(2,1)} %all-gather.6.cloned.1.call-done), kind=kOutput, calls=%fused_computation.30 | convolution fusion | flops 822083584 | bytes 8658944 | tf_op jit(solution)/shard_map/dot_general | solution.py:47
  228.0 3.3 %convolution_convert_fusion = bf16[4096,112]{0,1:T(8,128)(2,1)} fusion(bf16[4096,896]{1,0:T(8,128)(2,1)S(1)} %copy-done.2, bf16[112,896]{1,0:T(8,128)(2,1)S(1)} %copy-done.6), kind=kOutput, calls=%fused_computation.16 | convolution fusion | flops 822542336 | bytes 8458240 | tf_op jit(solution)/shard_map/dot_general | solution.py:46
  (30 shorter events, 0.1 us)
Async XLA Ops:
  7.2 49.0 %copy-start = (bf16[608,896]{1,0:T(8,128)(2,1)S(1)}, bf16[608,896]{1,0:T(8,128)(2,1)}, u32[]{:S(2)}) copy-start(bf16[608,896]{1,0:T(8,128)(2,1)} %param.18) | copy-start | bytes 3268612
  7.2 49.0 %all-gather.4.cloned.1.call-start = ((), (), s32[]{:S(2)}) async-start(), calls=%async_computation.1 | async-start | bytes 8257536 | tf_op jit(solution)/shard_map/all_gather | solution.py:28
  8.0 62.8 %copy-start.9 = (bf16[896,608]{0,1:T(8,128)(2,1)S(1)}, bf16[896,608]{0,1:T(8,128)(2,1)}, u32[]{:S(2)}) copy-start(bf16[896,608]{0,1:T(8,128)(2,1)} %param.16) | copy-start | bytes 3268612
  8.0 126.4 %reduce-scatter.2.cloned.1.call-start = ((), (), s32[]{:S(2)}) async-start(), calls=%async_computation.2 | async-start | bytes 8257536 | tf_op jit(solution)/shard_map/reduce_scatter | solution.py:41
  70.8 8.6 %copy-start.10 = (bf16[896,608]{0,1:T(8,128)(2,1)S(1)}, bf16[896,608]{0,1:T(8,128)(2,1)}, u32[]{:S(2)}) copy-start(bf16[896,608]{0,1:T(8,128)(2,1)} %param.17) | copy-start | bytes 3268612
  90.5 1.1 copy-start.7
  90.5 44.0 %copy-start.3 = (bf16[512,896]{1,0:T(8,128)(2,1)S(1)}, bf16[512,896]{1,0:T(8,128)(2,1)}, u32[]{:S(2)}) copy-start(bf16[512,896]{1,0:T(8,128)(2,1)} %param.19) | copy-start | bytes 2752516
  90.5 45.7 %copy-start.5 = (bf16[512,896]{1,0:T(8,128)(2,1)S(1)}, bf16[512,896]{1,0:T(8,128)(2,1)}, u32[]{:S(2)}) copy-start(bf16[512,896]{1,0:T(8,128)(2,1)} %param.21) | copy-start | bytes 2752516
  90.6 88.0 %all-gather.8.cloned.1.call-start = ((), (), s32[]{:S(2)}) async-start(), calls=%async_computation.4 | async-start | bytes 8257536 | tf_op jit(solution)/shard_map/all_gather | solution.py:27
  91.4 131.4 %all-gather.6.cloned.1.call-start = ((), (), s32[]{:S(2)}) async-start(), calls=%async_computation.3 | async-start | bytes 8257536 | tf_op jit(solution)/shard_map/all_gather | solution.py:45
  178.6 10.5 %copy-start.8 = (bf16[4096,896]{1,0:T(8,128)(2,1)S(1)}, bf16[4096,896]{1,0:T(8,128)(2,1)}, u32[]{:S(2)}) copy-start(bf16[4096,896]{1,0:T(8,128)(2,1)} %all-gather.8.cloned.1.call-done) | copy-start | bytes 22020100
  178.6 18.8 %slice-start = ((s8[7340032]{0:T(1024)(128)(4,1)}), s8[4194304]{0:T(1024)(128)(4,1)S(1)}, s32[]{:S(2)}) async-start(s8[7340032]{0:T(1024)(128)(4,1)} %bitcast.21), calls=%async_computation.5 | async-start | bytes 8388608
  178.6 18.8 %slice-start.2 = ((s8[4980736]{0:T(1024)(128)(4,1)}), s8[4194304]{0:T(1024)(128)(4,1)S(1)}, s32[]{:S(2)}) async-start(s8[4980736]{0:T(1024)(128)(4,1)} %bitcast.23), calls=%async_computation.7 | async-start | bytes 8388608
  178.6 18.8 %slice-start.4 = ((s8[4980736]{0:T(1024)(128)(4,1)}), s8[4194304]{0:T(1024)(128)(4,1)S(1)}, s32[]{:S(2)}) async-start(s8[4980736]{0:T(1024)(128)(4,1)} %bitcast.25), calls=%async_computation.9 | async-start | bytes 8388608
  189.0 8.3 %slice-start.1 = ((s8[7340032]{0:T(1024)(128)(4,1)}), s8[3145728]{0:T(1024)(128)(4,1)S(1)}, s32[]{:S(2)}) async-start(s8[7340032]{0:T(1024)(128)(4,1)} %bitcast.21), calls=%async_computation.6 | async-start | bytes 6291456
  189.0 8.4 %slice-start.3 = ((s8[4980736]{0:T(1024)(128)(4,1)}), s8[786432]{0:T(1024)(128)(4,1)S(1)}, s32[]{:S(2)}) async-start(s8[4980736]{0:T(1024)(128)(4,1)} %bitcast.23), calls=%async_computation.8 | async-start | bytes 1572864
  189.0 8.4 %slice-start.5 = ((s8[4980736]{0:T(1024)(128)(4,1)}), s8[786432]{0:T(1024)(128)(4,1)S(1)}, s32[]{:S(2)}) async-start(s8[4980736]{0:T(1024)(128)(4,1)} %bitcast.25), calls=%async_computation.10 | async-start | bytes 1572864
  197.4 25.3 %copy-start.4 = (bf16[4096,112]{0,1:T(8,128)(2,1)S(1)}, bf16[4096,112]{0,1:T(8,128)(2,1)}, u32[]{:S(2)}) copy-start(bf16[4096,112]{0,1:T(8,128)(2,1)} %param.22) | copy-start | bytes 2752516
  204.6 23.4 %copy-start.6 = (bf16[112,896]{1,0:T(8,128)(2,1)S(1)}, bf16[112,896]{1,0:T(8,128)(2,1)}, u32[]{:S(2)}) copy-start(bf16[112,896]{1,0:T(8,128)(2,1)} %param.23) | copy-start | bytes 602116
  222.8 5.3 %copy-start.2 = (bf16[4096,896]{1,0:T(8,128)(2,1)S(1)}, bf16[4096,896]{1,0:T(8,128)(2,1)}, u32[]{:S(2)}) copy-start(bf16[4096,896]{1,0:T(8,128)(2,1)} %all-gather.6.cloned.1.call-done) | copy-start | bytes 22020100
  222.8 8.6 %copy-start.1 = (bf16[608,896]{1,0:T(8,128)(2,1)S(1)}, bf16[608,896]{1,0:T(8,128)(2,1)}, u32[]{:S(2)}) copy-start(bf16[608,896]{1,0:T(8,128)(2,1)} %param.18) | copy-start | bytes 3268612
Sparse Core Ops, SparseCore 0:
  9.6 46.4 all-gather.3
  90.7 43.7 reduce-scatter.1
  136.1 42.4 all-gather.7
  180.6 42.1 all-gather.5
where the time goes:
time: 238 us
  waiting for transfers between devices  150 us (63%)
  matrix products  68.8 us (29%)
  between operations  13.9 us (6%)
  other arithmetic  4.5 us (2%)
    all_gather x1, waiting for transfers between devices, local_backward(): gy_full = lax.all_gather(grad_y, 'tp', axis=0, tiled=True)  48.1 us
    reduce_scatter x1, waiting for transfers between devices, local_backward(): lax.psum_scatter(part_x.astype(jnp.bfloat16), 'tp', scatter_dimension=0,...  42.8 us
    all_gather x1, waiting for transfers between devices, local_backward(): x_full = lax.all_gather(x_norm, 'tp', axis=0, tiled=True)  39.6 us
    all_gather x1, waiting for transfers between devices, local_backward(): gs_full = lax.all_gather(grad_sum, 'tp', axis=0, tiled=True)  18.1 us
    dot_general x1, matrix products, local_backward(): lax.dot_general(gy_full, w_down, CONTRACT_COLS, preferred_element_type=jn...  14.6 us
    dot_general x1, matrix products, local_backward(): lax.dot_general(grad_up, w_up, CONTRACT_COLS, preferred_element_type=jnp....  11.1 us
    dot_general x1, matrix products, local_backward(): lax.dot_general(x_full, grad_up, CONTRACT_ROWS, preferred_element_type=jn...  10.4 us
    dot_general x1, matrix products, local_backward(): lax.dot_general(grad_gate, w_gate, CONTRACT_COLS, preferred_element_type=...  8.57 us
  transfers between devices with their start and end apart: 4, of which 4 were waited for; matrix products, arithmetic and copies ran while one was open for 13% of the time, Pallas kernels for 0%

commit v1 on v0

v1 whole, which is shorter than its diff:
```python
import functools

import jax
import jax.numpy as jnp
from jax import lax
from jax.experimental import pallas as pl
from jax.experimental.pallas import tpu as pltpu
from jax.sharding import PartitionSpec as P

NORM_EPS = 1e-5
F32 = jnp.float32
BF16 = jnp.bfloat16
ROWS_ROWS = (((0,), (0,)), ((), ()))
COLS_COLS = (((1,), (1,)), ((), ()))
COLS_ROWS = (((1,), (0,)), ((), ()))
MESH = pl.DeviceIdType.MESH


def dot(a, b, dims):
    return lax.dot_general(a, b, dims, preferred_element_type=F32)


def kernel(tp, x_hbm, gy_hbm, ug_hbm, uu_hbm, wg_hbm, wu_hbm, wd_hbm, xin_hbm, gamma_ref, gr_hbm, o_hbm, wo_hbm,
           ds_out, do_out, dwg_out, dwu_out, dwd_out, dwo_out,
           gy, xb, part, peer, hop, froml, fromr, du, wgu, wd, wo, dwgu, dwd, dwo, ugb, uub, ob, dob, xin, gr,
           s_gy, r_gy, s_x, r_x, s_p, r_p, s_h, r_h, s_t, r_t, s_ds, r_ds,
           l_w, l_own, l_u, l_o, l_do, l_tok, l_out):
    half = gy.shape[1]
    cols = wd.shape[0]
    quarter = half // 2
    me = lax.axis_index("tp")
    core = lax.rem(me, 2)
    right = lax.rem(me + 2, tp)
    left = lax.rem(me + tp - 2, tp)
    partner = me + 1 - 2 * core

    def send(src, dst, ssem, rsem, dev):
        return pltpu.make_async_remote_copy(
            src_ref=src, dst_ref=dst, send_sem=ssem, recv_sem=rsem, device_id={"tp": dev}, device_id_type=MESH)

    def slot_row(k):
        g, b, i = k // 4, lax.rem(k, 4) // 2, lax.rem(k, 2)
        dx = jnp.where(g == 0, 0, jnp.where(g == 3, 2, 2 * i - 1))
        h = jnp.where(g == 2, 1 - i, i)
        chip = lax.rem(me // 2 + dx + tp // 2, tp // 2)
        shard = 2 * chip + lax.rem(core + b, 2)
        return pl.multiple_of((2 * shard + h) * half, half)

    def u_copies(k):
        tokens = pl.ds(slot_row(k), half)
        at = lax.rem(k, 2)
        return (pltpu.make_async_copy(ug_hbm.at[:, tokens], ugb.at[at], l_u.at[2 * at]),
                pltpu.make_async_copy(uu_hbm.at[:, tokens], uub.at[at], l_u.at[2 * at + 1]))

    def o_copy(n):
        tokens = pl.ds(pl.multiple_of(slot_row(n // 2) + lax.rem(n, 2) * quarter, quarter), quarter)
        return pltpu.make_async_copy(o_hbm.at[:, tokens], ob.at[n], l_o.at[n])

    def own(hbm, h):
        return hbm.at[pl.ds(h * half, half)]

    barrier = pltpu.get_barrier_semaphore()
    for dev in (left, right, partner):
        pl.semaphore_signal(barrier, inc=1, device_id={"tp": dev}, device_id_type=MESH)
    pl.semaphore_wait(barrier, 3)

    def send_own(hbm, buf, ssem, rsem):
        for src, dst, dev in ((0, 4, right), (1, 5, left), (1, 8, right), (0, 9, left), (0, 2, partner), (1, 3, partner)):
            send(own(hbm, src), buf.at[dst], ssem.at[dst], rsem.at[dst], dev).start()

    def arrived(buf, ssem, rsem, k):
        send(buf.at[k], buf.at[k], ssem.at[k], rsem.at[k], partner).wait_recv()

    def drain(buf, ssem, k):
        send(buf.at[k], buf.at[k], ssem.at[k], ssem.at[k], partner).wait_send()

    def gather_step(buf, ssem, rsem, k, also):
        place = lax.rem(k, 4)

        @pl.when((place == 0) & (k > 0))
        def _():
            arrived(buf, ssem, rsem, k)
            arrived(buf, ssem, rsem, k + 1)

            @pl.when(k == 4)
            def _():
                send(buf.at[4], buf.at[12], ssem.at[12], rsem.at[12], right).start()
                send(buf.at[5], buf.at[13], ssem.at[13], rsem.at[13], left).start()

            send(buf.at[k], buf.at[k + 2], ssem.at[k + 2], rsem.at[k + 2], partner).start()
            send(buf.at[k + 1], buf.at[k + 3], ssem.at[k + 3], rsem.at[k + 3], partner).start()
            if also is not None:
                pl.when(k == 4)(also)

        @pl.when(place >= 2)
        def _():
            arrived(buf, ssem, rsem, k)

    send_own(gy_hbm, gy, s_gy, r_gy)
    for h in range(2):
        pltpu.make_async_copy(own(gy_hbm, h), gy.at[h], l_own.at[h]).start()
        pltpu.make_async_copy(own(x_hbm, h), xb.at[h], l_own.at[2 + h]).start()
    weights = ((wd_hbm, wd), (wg_hbm, wgu.at[pl.ds(0, cols)]), (wu_hbm, wgu.at[pl.ds(cols, cols)]), (wo_hbm, wo))
    for i, (src, dst) in enumerate(weights):
        pltpu.make_async_copy(src, dst, l_w.at[i]).start()
    for c in u_copies(0):
        c.start()
    pltpu.make_async_copy(xin_hbm, xin, l_tok.at[0]).start()
    pltpu.make_async_copy(gr_hbm, gr, l_tok.at[1]).start()

    @pl.loop(0, 32)
    def _(n):
        o_copy(n).start()

    dwd[...] = jnp.zeros_like(dwd)
    dwgu[...] = jnp.zeros_like(dwgu)
    dwo[...] = jnp.zeros_like(dwo)
    for i, (src, dst) in enumerate(weights):
        pltpu.make_async_copy(src, dst, l_w.at[i]).wait()
    for h in range(2):
        pltpu.make_async_copy(own(gy_hbm, h), gy.at[h], l_own.at[h]).wait()
        pltpu.make_async_copy(own(x_hbm, h), xb.at[h], l_own.at[2 + h]).wait()

    def part_copy(k):
        j = (k // 4) * 2 + lax.rem(k, 2)
        return send(part.at[k], peer.at[j], s_p.at[j], r_p.at[j], partner)

    @pl.loop(0, 16)
    def _(k):
        @pl.when(k + 1 < 16)
        def _():
            for c in u_copies(k + 1):
                c.start()

        @pl.when((k > 0) & (lax.rem(k + 3, 4) >= 2))
        def _():
            part_copy(k - 1).start()

        gather_step(gy, s_gy, r_gy, k, lambda: send_own(x_hbm, xb, s_x, r_x))
        for c in u_copies(k):
            c.wait()
        at = lax.rem(k, 2)
        gyk = gy[k]
        gh = dot(wd[...], gyk, COLS_COLS)
        gate = ugb[at].astype(F32)
        up = uub[at].astype(F32)
        sig = jax.nn.sigmoid(gate)
        act = gate * sig
        silu = sig * (1.0 + gate * (1.0 - sig))
        z = (act * up).astype(BF16)
        du_up = (gh * act).astype(BF16)
        du_gate = (gh * up * silu).astype(BF16)
        du[k, pl.ds(0, cols)] = du_gate
        du[k, pl.ds(cols, cols)] = du_up
        dwd[...] += dot(z, gyk, COLS_ROWS)
        part[k] = dot(du[k], wgu[...], ROWS_ROWS).astype(BF16)

    part_copy(15).start()

    @pl.loop(2, 16)
    def _(k):
        drain(gy, s_gy, k)

    def add_peer(k, more=()):
        j = (k // 4) * 2 + k % 2
        t = part[k].astype(F32) + peer[j].astype(F32)
        for m in more:
            t = t + m[...].astype(F32)
        part[k] = t.astype(BF16)

    def q(ref, i):
        return ref.at[pl.ds(i * quarter, quarter)]

    def peer_arrived(j):
        send(peer.at[j], peer.at[j], s_p.at[j], r_p.at[j], partner).wait_recv()

    for j in range(8):
        peer_arrived(j)

    def hop_copy(k, i):
        side = k - 12
        return send(q(part.at[k], i), q(hop.at[side], i), s_h.at[2 * side + i], r_h.at[2 * side + i], (right, left)[side])

    for k in (12, 13):
        add_peer(k)
    for i in range(2):
        for k in (12, 13):
            hop_copy(k, i).start()

    def dw_step(j):
        xk = xb[pl.ds(2 * j, 2)].reshape(2 * half, xb.shape[2])
        duk = jnp.concatenate((du[2 * j], du[2 * j + 1]), axis=1)
        dwgu[...] += dot(duk, xk, COLS_ROWS)

    def tail_copy(side, qi):
        k = ((9, 5), (4, 8))[side][qi // 2]
        dst = (froml, fromr)[side].at[qi]
        return send(q(part.at[k], qi % 2), dst, s_t.at[4 * side + qi], r_t.at[4 * side + qi], (right, left)[side])

    tail_order = ((2, 0, 3, 1), (0, 2, 1, 3))

    def tails():
        add_peer(5)
        add_peer(4)
        for side in range(2):
            for i in range(2):
                hop_copy(12 + side, i).wait_recv()
        add_peer(9, (hop.at[0],))
        add_peer(8, (hop.at[1],))
        for n in range(4):
            for side in range(2):
                tail_copy(side, tail_order[side][n]).start()

    @pl.loop(0, 8)
    def _(j):
        pl.when(j == 6)(tails)
        gather_step(xb, s_x, r_x, 2 * j, None)

        @pl.when(lax.rem(j, 2) == 1)
        def _():
            arrived(xb, s_x, r_x, 2 * j + 1)

        dw_step(j)

    outs = ((dwgu.at[pl.ds(0, cols)], dwg_out), (dwgu.at[pl.ds(cols, cols)], dwu_out), (dwd, dwd_out))
    for i, (src, dst) in enumerate(outs):
        pltpu.make_async_copy(src, dst, l_out.at[i]).start()

    ds = gy
    pltpu.make_async_copy(xin_hbm, xin, l_tok.at[0]).wait()
    pltpu.make_async_copy(gr_hbm, gr, l_tok.at[1]).wait()
    gamma = gamma_ref[...].astype(F32)

    def norm_quarter(qi):
        h, i = qi // 2, qi % 2
        tail_copy(0, qi).wait_recv()
        tail_copy(1, qi).wait_recv()
        step = 32

        @pl.loop(0, quarter // step)
        def _(n):
            rows = pl.ds(pl.multiple_of(n * step, step), step)
            inner = pl.ds(pl.multiple_of(i * quarter + n * step, step), step)
            tokens = pl.ds(pl.multiple_of(qi * quarter + n * step, step), step)
            dx = (part[h, inner].astype(F32) + peer[h, inner].astype(F32)
                  + froml[qi, rows].astype(F32) + fromr[qi, rows].astype(F32)).astype(BF16)
            xf = xin[tokens].astype(F32)
            inv = lax.rsqrt(jnp.mean(xf * xf, axis=-1, keepdims=True) + NORM_EPS)
            scaled = dx.astype(F32) * gamma
            proj = jnp.mean(scaled * xf, axis=-1, keepdims=True)
            ds[h, inner] = (gr[tokens].astype(F32) + inv * (scaled - xf * (inv * inv) * proj)).astype(BF16)

    def ds_copy(src, dst, i, dev):
        n = 2 * dst + i
        return send(q(ds.at[src], i), q(ds.at[dst], i), s_ds.at[n], r_ds.at[n], dev)

    for i in range(2):
        for h in (0, 1):
            norm_quarter(2 * h + i)
        for src, dst, dev in ((0, 4, right), (1, 5, left), (1, 8, right), (0, 9, left), (0, 2, partner), (1, 3, partner)):
            ds_copy(src, dst, i, dev).start()
    for h in range(2):
        pltpu.make_async_copy(ds.at[h], ds_out.at[pl.ds(h * half, half)], l_out.at[4 + h]).start()

    @pl.loop(0, 32)
    def _(n):
        o_copy(n).wait()

    def do_copy(k, i):
        tokens = pl.ds(pl.multiple_of(slot_row(k) + i * quarter, quarter), quarter)
        return pltpu.make_async_copy(dob.at[2 * k + i], do_out.at[:, tokens], l_do.at[2 * k + i])

    @pl.loop(0, 16)
    def _(u):
        v, w = u - 4, u - 12
        i = jnp.where(u < 4, lax.rem(u, 2), jnp.where(u < 12, v // 4, w // 2))
        k = jnp.where(u < 4, 2 * (u // 2), jnp.where(u < 12, 4 + 2 * lax.rem(v, 4), 12 + 2 * lax.rem(w, 2)))

        @pl.when(k > 0)
        def _():
            for d in range(2):
                n = 2 * (k + d) + i
                block = q(ds.at[k + d], i)
                send(block, block, s_ds.at[n], r_ds.at[n], partner).wait_recv()

        @pl.when(k == 4)
        def _():
            for src, dst, dev in ((4, 12, right), (5, 13, left)):
                n = 2 * dst + i
                send(q(ds.at[src], i), q(ds.at[dst], i), s_ds.at[n], r_ds.at[n], dev).start()

        @pl.when((k > 0) & (lax.rem(k, 4) == 0))
        def _():
            for d in range(2):
                n = 2 * (k + 2 + d) + i
                send(q(ds.at[k + d], i), q(ds.at[k + 2 + d], i), s_ds.at[n], r_ds.at[n], partner).start()

        rows = pl.ds(pl.multiple_of(i * quarter, quarter), quarter)
        for d in range(2):
            block = ds[k + d, rows]
            n = 2 * (k + d) + i
            dob[n] = dot(wo[...], block, COLS_COLS).astype(BF16)
            dwo[...] += dot(ob[n], block, COLS_ROWS)
        for d in range(2):
            do_copy(k + d, i).start()

    pltpu.make_async_copy(dwo, dwo_out, l_out.at[3]).start()

    for i, (src, dst) in enumerate((*outs, (dwo, dwo_out))):
        pltpu.make_async_copy(src, dst, l_out.at[i]).wait()
    for h in range(2):
        pltpu.make_async_copy(ds.at[h], ds_out.at[pl.ds(h * half, half)], l_out.at[4 + h]).wait()

    @pl.loop(0, 32)
    def _(n):
        do_copy(n // 2, lax.rem(n, 2)).wait()

    @pl.loop(2, 16)
    def _(k):
        drain(xb, s_x, k)

    @pl.loop(4, 32)
    def _(n):
        block = q(ds.at[n // 2], 0)
        send(block, block, s_ds.at[n], s_ds.at[n], partner).wait_send()

    for j in range(8):
        send(peer.at[j], peer.at[j], s_p.at[j], s_p.at[j], partner).wait_send()
    for side in range(2):
        for i in range(2):
            hop_copy(12 + side, i).wait_send()
        for qi in range(4):
            tail_copy(side, qi).wait_send()


def solution(mesh):
    tp = mesh.shape["tp"]
    token_spec = P(("dp", "tp"), None)
    split_cols = P("dp", "tp")
    weight_cols = P(None, "tp")
    weight_rows = P("tp", None)

    def local_backward(x_norm, grad_y, u_gate, u_up, w_gate, w_up, w_down, x_in, gamma, grad_res, attn_out, w_out):
        rows, hid = x_norm.shape
        tokens, cols = u_gate.shape
        ocols = attn_out.shape[1]
        half = rows // 2
        quarter = half // 2
        any_spec = pl.BlockSpec(memory_space=pl.ANY)
        vmem_spec = pl.BlockSpec(memory_space=pltpu.VMEM)
        dma = pltpu.SemaphoreType.DMA
        ds, do, dwg, dwu, dwd, dwo = pl.pallas_call(
            functools.partial(kernel, tp),
            out_shape=(
                jax.ShapeDtypeStruct((rows, hid), BF16),
                jax.ShapeDtypeStruct((ocols, tokens), BF16),
                jax.ShapeDtypeStruct((cols, hid), F32),
                jax.ShapeDtypeStruct((cols, hid), F32),
                jax.ShapeDtypeStruct((cols, hid), F32),
                jax.ShapeDtypeStruct((ocols, hid), F32),
            ),
            in_specs=[any_spec] * 8 + [vmem_spec] + [any_spec] * 3,
            out_specs=(any_spec,) * 6,
            scratch_shapes=[
                pltpu.VMEM((16, half, hid), BF16),
                pltpu.VMEM((16, half, hid), BF16),
                pltpu.VMEM((16, half, hid), BF16),
                pltpu.VMEM((8, half, hid), BF16),
                pltpu.VMEM((2, half, hid), BF16),
                pltpu.VMEM((4, quarter, hid), BF16),
                pltpu.VMEM((4, quarter, hid), BF16),
                pltpu.VMEM((16, 2 * cols, half), BF16),
                pltpu.VMEM((2 * cols, hid), BF16),
                pltpu.VMEM((cols, hid), BF16),
                pltpu.VMEM((ocols, hid), BF16),
                pltpu.VMEM((2 * cols, hid), F32),
                pltpu.VMEM((cols, hid), F32),
                pltpu.VMEM((ocols, hid), F32),
                pltpu.VMEM((2, cols, half), BF16),
                pltpu.VMEM((2, cols, half), BF16),
                pltpu.VMEM((32, ocols, quarter), BF16),
                pltpu.VMEM((32, ocols, quarter), BF16),
                pltpu.VMEM((rows, hid), BF16),
                pltpu.VMEM((rows, hid), BF16),
                dma((16,)), dma((16,)),
                dma((16,)), dma((16,)),
                dma((8,)), dma((8,)),
                dma((4,)), dma((4,)),
                dma((8,)), dma((8,)),
                dma((32,)), dma((32,)),
                dma((4,)), dma((4,)), dma((4,)), dma((32,)), dma((32,)), dma((2,)), dma((6,)),
            ],
            compiler_params=pltpu.CompilerParams(
                collective_id=0, has_side_effects=True, vmem_limit_bytes=67_000_000),
            name="layer_backward",
        )(x_norm, grad_y, u_gate.T, u_up.T, w_gate.T, w_up.T, w_down, x_in, gamma.reshape(1, hid), grad_res, attn_out.T,
          w_out)
        return ds, do.T, dwg.T, dwu.T, dwd, dwo

    return jax.shard_map(
        local_backward,
        mesh=mesh,
        in_specs=(token_spec, token_spec, split_cols, split_cols, weight_cols, weight_cols, weight_rows,
                  token_spec, P(None), token_spec, split_cols, weight_rows),
        out_specs=(token_spec, split_cols, split_cols, split_cols, token_spec, token_spec),
        check_vma=False,
    )
```

time: 238 us -> 144 us (0.61)
  waiting for transfers between devices: 150 us -> 0 us
  Pallas kernels: 0 us -> 130 us
  matrix products: 68.8 us -> 0 us
  between operations: 13.9 us -> 0.65 us
  local copies, waits for them, and re-layouts: 0.08 us -> 12.7 us
  other arithmetic: 4.5 us -> 0 us
    pallas_call x0 -> x1, Pallas kernels: none -> 130 us  [local_backward(): pl.pallas_call(functools.partial(kernel, tp), out_shape=(jax.ShapeDtypeSt...]
    all_gather x3 -> x0, waiting for transfers between devices: 106 us -> none  [the longest x1 48.1 us: local_backward(): gy_full = lax.all_gather(grad_y, 'tp', axis=0, tiled=True)]
    dot_general x8 -> x0, matrix products: 68.8 us -> none  [the longest x1 14.6 us: local_backward(): lax.dot_general(gy_full, w_down, CONTRACT_COLS, preferred_element_type=jn...]
    reduce_scatter x1 -> x0, waiting for transfers between devices: 42.8 us -> none  [local_backward(): lax.psum_scatter(part_x.astype(jnp.bfloat16), 'tp', scatter_dimension=0,...]
    unnamed x34 -> x14, local copies, waits for them, and re-layouts: 0.08 us -> 11.4 us
    convert_element_type x2 -> x0, other arithmetic: 2.8 us -> none  [the longest x1 2.8 us: rms_backward(): return (grad_res.astype(jnp.float32) + inv_rms * (scaled - xin_f * (inv_r...]
  transfers between devices with their start and end apart: 4 -> 0, of which waited for: 4 -> 0; matrix products, arithmetic and copies ran while one was open for 13% -> 0% of each run, Pallas kernels for 0% -> 0%
where the time goes in v1:
time: 144 us; the launch traced here: 143 us
  Pallas kernels  130 us (90%)
  local copies, waits for them, and re-layouts  12.7 us (9%)
    pallas_call x1, Pallas kernels, local_backward(): pl.pallas_call(functools.partial(kernel, tp), out_shape=(jax.ShapeDtypeSt...  130 us
    unnamed x14, local copies, waits for them, and re-layouts  11.4 us

profile of v1, /device:TPU:81, one launch (start us, length us, event | category | flops | bytes accessed | tf_op | source)
XLA Modules:
  0.0 143.4 jit_solution(17267173748166917212)
XLA Ops:
  0.6 1.3 reshape.15.gamma_ref
  1.9 130.1 %layer_backward.1 = (bf16[512,896]{1,0:T(8,128)(2,1)}, bf16[112,4096]{1,0:T(8,128)(2,1)}, f32[608,896]{1,0:T(8,128)}, f32[608,896]{1,0:T(8,128)}, f32[608,896]{1,0:T(8,128)}, /*index=5*/f32[112,896]{1,0:T(8,128)}) custom-call(bf16[512,896]{1,0:T(8,128)(2,1)} %x_hbm.1, bf16[512,896]{1,0:T(8,128)(2,1)} %gy_hbm.1, bf16[608,4096]{1,0:T(8,128)(2,1)} %bitcast.8, ...), custom_call_target="tpu_custom_call" | custom-call | tf_op jit(solution)/shard_map/layer_backward/pallas_call | solution.py:352
  132.0 0.0 copy-start.2
  132.0 2.3 %copy.24 = bf16[512,896]{1,0:T(8,128)(2,1)} copy(bf16[512,896]{1,0:T(8,128)(2,1)} %get-tuple-element.24) | data formatting | bytes 1835008
  134.3 2.2 %copy.25 = bf16[4096,112]{0,1:T(8,128)(2,1)} copy(bf16[4096,112]{0,1:T(8,128)(2,1)} %bitcast.14) | data formatting | bytes 1835008
  136.5 0.0 copy-done.2
  136.5 0.0 copy-start.1
  136.5 1.3 copy.26
  137.8 1.1 copy-done.1
  138.9 0.0 copy-start
  138.9 1.3 copy.27
  140.2 1.1 copy-done
  141.3 0.0 copy-start.3
  141.3 1.3 copy.28
  142.6 0.0 copy-done.3
  142.6 0.7 copy.29
Async XLA Ops:
  132.0 4.5 %copy-start.2 = (f32[608,896]{1,0:T(8,128)S(1)}, f32[608,896]{1,0:T(8,128)}, u32[]{:S(2)}) copy-start(f32[608,896]{1,0:T(8,128)} %get-tuple-element.14) | copy-start | bytes 6537220
  136.5 2.4 %copy-start.1 = (f32[608,896]{1,0:T(8,128)S(1)}, f32[608,896]{1,0:T(8,128)}, u32[]{:S(2)}) copy-start(f32[608,896]{1,0:T(8,128)} %get-tuple-element.15) | copy-start | bytes 6537220
  138.9 2.4 %copy-start = (f32[608,896]{1,0:T(8,128)S(1)}, f32[608,896]{1,0:T(8,128)}, u32[]{:S(2)}) copy-start(f32[608,896]{1,0:T(8,128)} %get-tuple-element.28) | copy-start | bytes 6537220
  141.3 1.4 copy-start.3

commit v2 on v1

--- a/solution.py
+++ b/solution.py
@@ -20,31 +20,58 @@
     return lax.dot_general(a, b, dims, preferred_element_type=F32)
 
 
+def slot_token(tp, half, k):
+    me = lax.axis_index("tp")
+    g, b, i = k // 4, lax.rem(k, 4) // 2, lax.rem(k, 2)
+    dx = jnp.where(g == 0, 0, jnp.where(g == 3, 2, 2 * i - 1))
+    h = jnp.where(g == 2, 1 - i, i)
+    chip = lax.rem(me // 2 + dx + tp // 2, tp // 2)
+    shard = 2 * chip + lax.rem(lax.rem(me, 2) + b, 2)
+    return pl.multiple_of((2 * shard + h) * half, half)
+
+
+def write_kernel(tp, half, dso, dob, dwgu, dwd, dwo, ds_out, do_out, dwg_out, dwu_out, dwd_out, dwo_out, sem, sem_do):
+    cols, quarter = dwd.shape[0], half // 2
+    copies = [pltpu.make_async_copy(src, dst, sem.at[i]) for i, (src, dst) in enumerate((
+        (dwgu.at[pl.ds(0, cols)], dwg_out), (dwgu.at[pl.ds(cols, cols)], dwu_out), (dwd, dwd_out), (dso, ds_out),
+        (dwo, dwo_out)))]
+
+    def do_copy(n):
+        tokens = pl.ds(pl.multiple_of(slot_token(tp, half, n // 2) + lax.rem(n, 2) * quarter, quarter), quarter)
+        return pltpu.make_async_copy(dob.at[n], do_out.at[:, tokens], sem_do.at[n])
+
+    for c in copies:
+        c.start()
+
+    @pl.loop(0, 2 * 2 * tp)
+    def _(n):
+        do_copy(n).start()
+
+    @pl.loop(0, 2 * 2 * tp)
+    def _(n):
+        do_copy(n).wait()
+
+    for c in copies:
+        c.wait()
+
+
 def kernel(tp, x_hbm, gy_hbm, ug_hbm, uu_hbm, wg_hbm, wu_hbm, wd_hbm, xin_hbm, gamma_ref, gr_hbm, o_hbm, wo_hbm,
-           ds_out, do_out, dwg_out, dwu_out, dwd_out, dwo_out,
-           gy, xb, part, peer, hop, froml, fromr, du, wgu, wd, wo, dwgu, dwd, dwo, ugb, uub, ob, dob, xin, gr,
+           dso, dob, dwgu, dwd, dwo,
+           gy, xb, part, peer, hop, froml, fromr, du, wgu, wd, wo, ugb, uub, ob, xin, gr,
            s_gy, r_gy, s_x, r_x, s_p, r_p, s_h, r_h, s_t, r_t, s_ds, r_ds,
-           l_w, l_own, l_u, l_o, l_do, l_tok, l_out):
+           l_w, l_own, l_u, l_o, l_tok):
     half = gy.shape[1]
     cols = wd.shape[0]
     quarter = half // 2
     me = lax.axis_index("tp")
-    core = lax.rem(me, 2)
     right = lax.rem(me + 2, tp)
     left = lax.rem(me + tp - 2, tp)
-    partner = me + 1 - 2 * core
+    partner = me + 1 - 2 * lax.rem(me, 2)
+    slot_row = functools.partial(slot_token, tp, half)
 
     def send(src, dst, ssem, rsem, dev):
         return pltpu.make_async_remote_copy(
             src_ref=src, dst_ref=dst, send_sem=ssem, recv_sem=rsem, device_id={"tp": dev}, device_id_type=MESH)
-
-    def slot_row(k):
-        g, b, i = k // 4, lax.rem(k, 4) // 2, lax.rem(k, 2)
-        dx = jnp.where(g == 0, 0, jnp.where(g == 3, 2, 2 * i - 1))
-        h = jnp.where(g == 2, 1 - i, i)
-        chip = lax.rem(me // 2 + dx + tp // 2, tp // 2)
-        shard = 2 * chip + lax.rem(core + b, 2)
-        return pl.multiple_of((2 * shard + h) * half, half)
 
     def u_copies(k):
         tokens = pl.ds(slot_row(k), half)
@@ -222,14 +249,10 @@
 
         dw_step(j)
 
-    outs = ((dwgu.at[pl.ds(0, cols)], dwg_out), (dwgu.at[pl.ds(cols, cols)], dwu_out), (dwd, dwd_out))
-    for i, (src, dst) in enumerate(outs):
-        pltpu.make_async_copy(src, dst, l_out.at[i]).start()
-
     ds = gy
     pltpu.make_async_copy(xin_hbm, xin, l_tok.at[0]).wait()
     pltpu.make_async_copy(gr_hbm, gr, l_tok.at[1]).wait()
-    gamma = gamma_ref[...].astype(F32)
+    gamma = gamma_ref[...].astype(F32).reshape(1, gamma_ref.shape[0])
 
     def norm_quarter(qi):
         h, i = qi // 2, qi % 2
@@ -248,7 +271,9 @@
             inv = lax.rsqrt(jnp.mean(xf * xf, axis=-1, keepdims=True) + NORM_EPS)
             scaled = dx.astype(F32) * gamma
             proj = jnp.mean(scaled * xf, axis=-1, keepdims=True)
-            ds[h, inner] = (gr[tokens].astype(F32) + inv * (scaled - xf * (inv * inv) * proj)).astype(BF16)
+            out = (gr[tokens].astype(F32) + inv * (scaled - xf * (inv * inv) * proj)).astype(BF16)
+            ds[h, inner] = out
+            dso[tokens] = out
 
     def ds_copy(src, dst, i, dev):
         n = 2 * dst + i
@@ -259,16 +284,10 @@
             norm_quarter(2 * h + i)
         for src, dst, dev in ((0, 4, right), (1, 5, left), (1, 8, right), (0, 9, left), (0, 2, partner), (1, 3, partner)):
             ds_copy(src, dst, i, dev).start()
-    for h in range(2):
-        pltpu.make_async_copy(ds.at[h], ds_out.at[pl.ds(h * half, half)], l_out.at[4 + h]).start()
 
     @pl.loop(0, 32)
     def _(n):
         o_copy(n).wait()
-
-    def do_copy(k, i):
-        tokens = pl.ds(pl.multiple_of(slot_row(k) + i * quarter, quarter), quarter)
-        return pltpu.make_async_copy(dob.at[2 * k + i], do_out.at[:, tokens], l_do.at[2 * k + i])
 
     @pl.loop(0, 16)
     def _(u):
@@ -301,19 +320,6 @@
             n = 2 * (k + d) + i
             dob[n] = dot(wo[...], block, COLS_COLS).astype(BF16)
             dwo[...] += dot(ob[n], block, COLS_ROWS)
-        for d in range(2):
-            do_copy(k + d, i).start()
-
-    pltpu.make_async_copy(dwo, dwo_out, l_out.at[3]).start()
-
-    for i, (src, dst) in enumerate((*outs, (dwo, dwo_out))):
-        pltpu.make_async_copy(src, dst, l_out.at[i]).wait()
-    for h in range(2):
-        pltpu.make_async_copy(ds.at[h], ds_out.at[pl.ds(h * half, half)], l_out.at[4 + h]).wait()
-
-    @pl.loop(0, 32)
-    def _(n):
-        do_copy(n // 2, lax.rem(n, 2)).wait()
 
     @pl.loop(2, 16)
     def _(k):
@@ -349,18 +355,17 @@
         any_spec = pl.BlockSpec(memory_space=pl.ANY)
         vmem_spec = pl.BlockSpec(memory_space=pltpu.VMEM)
         dma = pltpu.SemaphoreType.DMA
-        ds, do, dwg, dwu, dwd, dwo = pl.pallas_call(
+        results = pl.pallas_call(
             functools.partial(kernel, tp),
             out_shape=(
-                jax.ShapeDtypeStruct((rows, hid), BF16),
-                jax.ShapeDtypeStruct((ocols, tokens), BF16),
-                jax.ShapeDtypeStruct((cols, hid), F32),
-                jax.ShapeDtypeStruct((cols, hid), F32),
-                jax.ShapeDtypeStruct((cols, hid), F32),
-                jax.ShapeDtypeStruct((ocols, hid), F32),
+                pltpu.VMEM((rows, hid), BF16),
+                pltpu.VMEM((32, ocols, quarter), BF16),
+                pltpu.VMEM((2 * cols, hid), F32),
+                pltpu.VMEM((cols, hid), F32),
+                pltpu.VMEM((ocols, hid), F32),
             ),
             in_specs=[any_spec] * 8 + [vmem_spec] + [any_spec] * 3,
-            out_specs=(any_spec,) * 6,
+            out_specs=(vmem_spec,) * 5,
             scratch_shapes=[
                 pltpu.VMEM((16, half, hid), BF16),
                 pltpu.VMEM((16, half, hid), BF16),
@@ -373,12 +378,8 @@
                 pltpu.VMEM((2 * cols, hid), BF16),
                 pltpu.VMEM((cols, hid), BF16),
                 pltpu.VMEM((ocols, hid), BF16),
-                pltpu.VMEM((2 * cols, hid), F32),
-                pltpu.VMEM((cols, hid), F32),
-                pltpu.VMEM((ocols, hid), F32),
                 pltpu.VMEM((2, cols, half), BF16),
                 pltpu.VMEM((2, cols, half), BF16),
-                pltpu.VMEM((32, ocols, quarter), BF16),
                 pltpu.VMEM((32, ocols, quarter), BF16),
                 pltpu.VMEM((rows, hid), BF16),
                 pltpu.VMEM((rows, hid), BF16),
@@ -388,13 +389,30 @@
                 dma((4,)), dma((4,)),
                 dma((8,)), dma((8,)),
                 dma((32,)), dma((32,)),
-                dma((4,)), dma((4,)), dma((4,)), dma((32,)), dma((32,)), dma((2,)), dma((6,)),
+                dma((4,)), dma((4,)), dma((4,)), dma((32,)), dma((2,)),
             ],
             compiler_params=pltpu.CompilerParams(
-                collective_id=0, has_side_effects=True, vmem_limit_bytes=67_000_000),
+                collective_id=0, has_side_effects=True, vmem_limit_bytes=54_000_000),
             name="layer_backward",
-        )(x_norm, grad_y, u_gate.T, u_up.T, w_gate.T, w_up.T, w_down, x_in, gamma.reshape(1, hid), grad_res, attn_out.T,
+        )(x_norm, grad_y, u_gate.T, u_up.T, w_gate.T, w_up.T, w_down, x_in, gamma, grad_res, attn_out.T,
           w_out)
+        results = [pltpu.with_memory_space_constraint(r, pltpu.VMEM) for r in results]
+        ds, do, dwg, dwu, dwd, dwo = pl.pallas_call(
+            functools.partial(write_kernel, tp, half),
+            out_shape=(
+                jax.ShapeDtypeStruct((rows, hid), BF16),
+                jax.ShapeDtypeStruct((ocols, tokens), BF16),
+                jax.ShapeDtypeStruct((cols, hid), F32),
+                jax.ShapeDtypeStruct((cols, hid), F32),
+                jax.ShapeDtypeStruct((cols, hid), F32),
+                jax.ShapeDtypeStruct((ocols, hid), F32),
+            ),
+            in_specs=[vmem_spec] * 5,
+            out_specs=(any_spec,) * 6,
+            scratch_shapes=[dma((5,)), dma((32,))],
+            compiler_params=pltpu.CompilerParams(vmem_limit_bytes=1_000_000),
+            name="write_results",
+        )(*results)
         return ds, do.T, dwg.T, dwu.T, dwd, dwo
 
     return jax.shard_map(

time: 144 us -> 133 us (0.924)
  local copies, waits for them, and re-layouts: 12.7 us -> 0 us
  Pallas kernels: 130 us -> 132 us
    unnamed x14 -> x0, local copies, waits for them, and re-layouts: 11.4 us -> none
    pallas_call x1 -> x2, Pallas kernels: 130 us -> 132 us  [the longest x1 129 us: local_backward(): pl.pallas_call(functools.partial(kernel, tp), out_shape=(pltpu.VMEM((rows...]
where the time goes in v2:
time: 133 us
  Pallas kernels  132 us (99%)
    pallas_call x1, Pallas kernels, local_backward(): pl.pallas_call(functools.partial(kernel, tp), out_shape=(pltpu.VMEM((rows...  129 us
    pallas_call x1, Pallas kernels, local_backward(): pl.pallas_call(functools.partial(write_kernel, tp, half), out_shape=(jax....  3.7 us

profile of v2, /device:TPU:81, one launch (start us, length us, event | category | flops | bytes accessed | tf_op | source)
XLA Modules:
  0.0 132.9 jit_solution(14908316853219115639)
XLA Ops:
  0.6 128.6 %layer_backward.1 = (bf16[512,896]{1,0:T(8,128)(2,1)S(1)}, bf16[32,112,128]{2,1,0:T(8,128)(2,1)S(1)}, f32[1216,896]{1,0:T(8,128)S(1)}, f32[608,896]{1,0:T(8,128)S(1)}, f32[112,896]{1,0:T(8,128)S(1)}) custom-call(bf16[512,896]{1,0:T(8,128)(2,1)} %x_hbm.1, bf16[512,896]{1,0:T(8,128)(2,1)} %gy_hbm.1, bf16[608,4096]{1,0:T(8,128)(2,1)} %bitcast.8, ...), custom_call_target="tpu_custom_call" | custom-call | tf_op jit(solution)/shard_map/layer_backward/pallas_call | solution.py:358
  129.2 3.7 %write_results.1 = (bf16[512,896]{1,0:T(8,128)(2,1)}, bf16[112,4096]{1,0:T(8,128)(2,1)}, f32[608,896]{1,0:T(8,128)}, f32[608,896]{1,0:T(8,128)}, f32[608,896]{1,0:T(8,128)}, /*index=5*/f32[112,896]{1,0:T(8,128)}) custom-call(bf16[512,896]{1,0:T(8,128)(2,1)S(1)} %get-tuple-element.17.dso, bf16[32,112,128]{2,1,0:T(8,128)(2,1)S(1)} %get-tuple-element.18.dob, ...), custom_call_target="tpu_custom_call" | custom-call | tf_op jit(solution)/shard_map/write_results/pallas_call | solution.py:400

commit v3 on v2

--- a/solution.py
+++ b/solution.py
@@ -86,14 +86,9 @@
     def own(hbm, h):
         return hbm.at[pl.ds(h * half, half)]
 
-    barrier = pltpu.get_barrier_semaphore()
-    for dev in (left, right, partner):
-        pl.semaphore_signal(barrier, inc=1, device_id={"tp": dev}, device_id_type=MESH)
-    pl.semaphore_wait(barrier, 3)
-
-    def send_own(hbm, buf, ssem, rsem):
+    def send_own(buf, ssem, rsem):
         for src, dst, dev in ((0, 4, right), (1, 5, left), (1, 8, right), (0, 9, left), (0, 2, partner), (1, 3, partner)):
-            send(own(hbm, src), buf.at[dst], ssem.at[dst], rsem.at[dst], dev).start()
+            send(buf.at[src], buf.at[dst], ssem.at[dst], rsem.at[dst], dev).start()
 
     def arrived(buf, ssem, rsem, k):
         send(buf.at[k], buf.at[k], ssem.at[k], rsem.at[k], partner).wait_recv()
@@ -123,15 +118,22 @@
         def _():
             arrived(buf, ssem, rsem, k)
 
-    send_own(gy_hbm, gy, s_gy, r_gy)
+    barrier = pltpu.get_barrier_semaphore()
+    for dev in (left, right, partner):
+        pl.semaphore_signal(barrier, inc=1, device_id={"tp": dev}, device_id_type=MESH)
     for h in range(2):
         pltpu.make_async_copy(own(gy_hbm, h), gy.at[h], l_own.at[h]).start()
-        pltpu.make_async_copy(own(x_hbm, h), xb.at[h], l_own.at[2 + h]).start()
     weights = ((wd_hbm, wd), (wg_hbm, wgu.at[pl.ds(0, cols)]), (wu_hbm, wgu.at[pl.ds(cols, cols)]), (wo_hbm, wo))
     for i, (src, dst) in enumerate(weights):
         pltpu.make_async_copy(src, dst, l_w.at[i]).start()
     for c in u_copies(0):
         c.start()
+    for h in range(2):
+        pltpu.make_async_copy(own(x_hbm, h), xb.at[h], l_own.at[2 + h]).start()
+    for h in range(2):
+        pltpu.make_async_copy(own(gy_hbm, h), gy.at[h], l_own.at[h]).wait()
+    pl.semaphore_wait(barrier, 3)
+    send_own(gy, s_gy, r_gy)
     pltpu.make_async_copy(xin_hbm, xin, l_tok.at[0]).start()
     pltpu.make_async_copy(gr_hbm, gr, l_tok.at[1]).start()
 
@@ -145,7 +147,6 @@
     for i, (src, dst) in enumerate(weights):
         pltpu.make_async_copy(src, dst, l_w.at[i]).wait()
     for h in range(2):
-        pltpu.make_async_copy(own(gy_hbm, h), gy.at[h], l_own.at[h]).wait()
         pltpu.make_async_copy(own(x_hbm, h), xb.at[h], l_own.at[2 + h]).wait()
 
     def part_copy(k):
@@ -163,7 +164,7 @@
         def _():
             part_copy(k - 1).start()
 
-        gather_step(gy, s_gy, r_gy, k, lambda: send_own(x_hbm, xb, s_x, r_x))
+        gather_step(gy, s_gy, r_gy, k, lambda: send_own(xb, s_x, r_x))
         for c in u_copies(k):
             c.wait()
         at = lax.rem(k, 2)

time: 133 us -> 134 us (level)
  no operation moved by 1% of the time
where the time goes in v3:
time: 134 us
  Pallas kernels  133 us (99%)
    pallas_call x1, Pallas kernels, local_backward(): pl.pallas_call(functools.partial(kernel, tp), out_shape=(pltpu.VMEM((rows...  129 us
    pallas_call x1, Pallas kernels, local_backward(): pl.pallas_call(functools.partial(write_kernel, tp, half), out_shape=(jax....  3.7 us

profile of v3, /device:TPU:81, one launch (start us, length us, event | category | flops | bytes accessed | tf_op | source)
XLA Modules:
  0.0 133.8 jit_solution(7874465583632409908)
XLA Ops:
  0.6 129.5 %layer_backward.1 = (bf16[512,896]{1,0:T(8,128)(2,1)S(1)}, bf16[32,112,128]{2,1,0:T(8,128)(2,1)S(1)}, f32[1216,896]{1,0:T(8,128)S(1)}, f32[608,896]{1,0:T(8,128)S(1)}, f32[112,896]{1,0:T(8,128)S(1)}) custom-call(bf16[512,896]{1,0:T(8,128)(2,1)} %x_hbm.1, bf16[512,896]{1,0:T(8,128)(2,1)} %gy_hbm.1, bf16[608,4096]{1,0:T(8,128)(2,1)} %bitcast.8, ...), custom_call_target="tpu_custom_call" | custom-call | tf_op jit(solution)/shard_map/layer_backward/pallas_call | solution.py:359
  130.1 3.7 %write_results.1 = (bf16[512,896]{1,0:T(8,128)(2,1)}, bf16[112,4096]{1,0:T(8,128)(2,1)}, f32[608,896]{1,0:T(8,128)}, f32[608,896]{1,0:T(8,128)}, f32[608,896]{1,0:T(8,128)}, /*index=5*/f32[112,896]{1,0:T(8,128)}) custom-call(bf16[512,896]{1,0:T(8,128)(2,1)S(1)} %get-tuple-element.17.dso, bf16[32,112,128]{2,1,0:T(8,128)(2,1)S(1)} %get-tuple-element.18.dob, ...), custom_call_target="tpu_custom_call" | custom-call | tf_op jit(solution)/shard_map/write_results/pallas_call | solution.py:401

commit v4 on v3

--- a/solution.py
+++ b/solution.py
@@ -123,6 +123,10 @@
         pl.semaphore_signal(barrier, inc=1, device_id={"tp": dev}, device_id_type=MESH)
     for h in range(2):
         pltpu.make_async_copy(own(gy_hbm, h), gy.at[h], l_own.at[h]).start()
+    pl.semaphore_wait(barrier, 3)
+    for h in range(2):
+        pltpu.make_async_copy(own(gy_hbm, h), gy.at[h], l_own.at[h]).wait()
+    send_own(gy, s_gy, r_gy)
     weights = ((wd_hbm, wd), (wg_hbm, wgu.at[pl.ds(0, cols)]), (wu_hbm, wgu.at[pl.ds(cols, cols)]), (wo_hbm, wo))
     for i, (src, dst) in enumerate(weights):
         pltpu.make_async_copy(src, dst, l_w.at[i]).start()
@@ -130,10 +134,6 @@
         c.start()
     for h in range(2):
         pltpu.make_async_copy(own(x_hbm, h), xb.at[h], l_own.at[2 + h]).start()
-    for h in range(2):
-        pltpu.make_async_copy(own(gy_hbm, h), gy.at[h], l_own.at[h]).wait()
-    pl.semaphore_wait(barrier, 3)
-    send_own(gy, s_gy, r_gy)
     pltpu.make_async_copy(xin_hbm, xin, l_tok.at[0]).start()
     pltpu.make_async_copy(gr_hbm, gr, l_tok.at[1]).start()
 

time: 134 us -> 134 us (level)
  no operation moved by 1% of the time
where the time goes in v4:
time: 134 us; the launch traced here: 133 us
  Pallas kernels  133 us (99%)
    pallas_call x1, Pallas kernels, local_backward(): pl.pallas_call(functools.partial(kernel, tp), out_shape=(pltpu.VMEM((rows...  129 us
    pallas_call x1, Pallas kernels, local_backward(): pl.pallas_call(functools.partial(write_kernel, tp, half), out_shape=(jax....  3.7 us

profile of v4, /device:TPU:81, one launch (start us, length us, event | category | flops | bytes accessed | tf_op | source)
XLA Modules:
  0.0 133.5 jit_solution(6166977188115315765)
XLA Ops:
  0.6 129.1 %layer_backward.1 = (bf16[512,896]{1,0:T(8,128)(2,1)S(1)}, bf16[32,112,128]{2,1,0:T(8,128)(2,1)S(1)}, f32[1216,896]{1,0:T(8,128)S(1)}, f32[608,896]{1,0:T(8,128)S(1)}, f32[112,896]{1,0:T(8,128)S(1)}) custom-call(bf16[512,896]{1,0:T(8,128)(2,1)} %x_hbm.1, bf16[512,896]{1,0:T(8,128)(2,1)} %gy_hbm.1, bf16[608,4096]{1,0:T(8,128)(2,1)} %bitcast.8, ...), custom_call_target="tpu_custom_call" | custom-call | tf_op jit(solution)/shard_map/layer_backward/pallas_call | solution.py:359
  129.8 3.7 %write_results.1 = (bf16[512,896]{1,0:T(8,128)(2,1)}, bf16[112,4096]{1,0:T(8,128)(2,1)}, f32[608,896]{1,0:T(8,128)}, f32[608,896]{1,0:T(8,128)}, f32[608,896]{1,0:T(8,128)}, /*index=5*/f32[112,896]{1,0:T(8,128)}) custom-call(bf16[512,896]{1,0:T(8,128)(2,1)S(1)} %get-tuple-element.17.dso, bf16[32,112,128]{2,1,0:T(8,128)(2,1)S(1)} %get-tuple-element.18.dob, ...), custom_call_target="tpu_custom_call" | custom-call | tf_op jit(solution)/shard_map/write_results/pallas_call | solution.py:401

commit v5 on v2

--- a/solution.py
+++ b/solution.py
@@ -66,7 +66,8 @@
     me = lax.axis_index("tp")
     right = lax.rem(me + 2, tp)
     left = lax.rem(me + tp - 2, tp)
-    partner = me + 1 - 2 * lax.rem(me, 2)
+    core = lax.rem(me, 2)
+    partner = me + 1 - 2 * core
     slot_row = functools.partial(slot_token, tp, half)
 
     def send(src, dst, ssem, rsem, dev):
@@ -91,8 +92,9 @@
         pl.semaphore_signal(barrier, inc=1, device_id={"tp": dev}, device_id_type=MESH)
     pl.semaphore_wait(barrier, 3)
 
-    def send_own(hbm, buf, ssem, rsem):
-        for src, dst, dev in ((0, 4, right), (1, 5, left), (1, 8, right), (0, 9, left), (0, 2, partner), (1, 3, partner)):
+    def send_own(hbm, buf, ssem, rsem, first=0):
+        plan = ((0, 4, right), (1, 5, left), (1, 8, right), (0, 9, left), (0, 2, partner), (1, 3, partner))
+        for src, dst, dev in plan[first:]:
             send(own(hbm, src), buf.at[dst], ssem.at[dst], rsem.at[dst], dev).start()
 
     def arrived(buf, ssem, rsem, k):
@@ -123,7 +125,19 @@
         def _():
             arrived(buf, ssem, rsem, k)
 
-    send_own(gy_hbm, gy, s_gy, r_gy)
+    cut = quarter // 2
+
+    @pl.when(core == 0)
+    def _():
+        send_own(gy_hbm, gy, s_gy, r_gy)
+
+    @pl.when(core == 1)
+    def _():
+        for src, dst, dev in ((0, 4, right), (1, 5, left)):
+            for lo, n in ((0, cut), (cut, half - cut)):
+                send(gy_hbm.at[pl.ds(src * half + lo, n)], gy.at[dst, pl.ds(lo, n)], s_gy.at[dst], r_gy.at[dst], dev).start()
+        send_own(gy_hbm, gy, s_gy, r_gy, 2)
+
     for h in range(2):
         pltpu.make_async_copy(own(gy_hbm, h), gy.at[h], l_own.at[h]).start()
         pltpu.make_async_copy(own(x_hbm, h), xb.at[h], l_own.at[2 + h]).start()

time: 133 us -> 133 us (level)
  no operation moved by 1% of the time
where the time goes in v5:
time: 133 us
  Pallas kernels  132 us (99%)
    pallas_call x1, Pallas kernels, local_backward(): pl.pallas_call(functools.partial(kernel, tp), out_shape=(pltpu.VMEM((rows...  129 us
    pallas_call x1, Pallas kernels, local_backward(): pl.pallas_call(functools.partial(write_kernel, tp, half), out_shape=(jax....  3.7 us

profile of v5, /device:TPU:81, one launch (start us, length us, event | category | flops | bytes accessed | tf_op | source)
XLA Modules:
  0.0 132.9 jit_solution(4875390672895243835)
XLA Ops:
  0.6 128.6 %layer_backward.1 = (bf16[512,896]{1,0:T(8,128)(2,1)S(1)}, bf16[32,112,128]{2,1,0:T(8,128)(2,1)S(1)}, f32[1216,896]{1,0:T(8,128)S(1)}, f32[608,896]{1,0:T(8,128)S(1)}, f32[112,896]{1,0:T(8,128)S(1)}) custom-call(bf16[512,896]{1,0:T(8,128)(2,1)} %x_hbm.1, bf16[512,896]{1,0:T(8,128)(2,1)} %gy_hbm.1, bf16[608,4096]{1,0:T(8,128)(2,1)} %bitcast.8, ...), custom_call_target="tpu_custom_call" | custom-call | tf_op jit(solution)/shard_map/layer_backward/pallas_call | solution.py:372
  129.2 3.7 %write_results.1 = (bf16[512,896]{1,0:T(8,128)(2,1)}, bf16[112,4096]{1,0:T(8,128)(2,1)}, f32[608,896]{1,0:T(8,128)}, f32[608,896]{1,0:T(8,128)}, f32[608,896]{1,0:T(8,128)}, /*index=5*/f32[112,896]{1,0:T(8,128)}) custom-call(bf16[512,896]{1,0:T(8,128)(2,1)S(1)} %get-tuple-element.17.dso, bf16[32,112,128]{2,1,0:T(8,128)(2,1)S(1)} %get-tuple-element.18.dob, ...), custom_call_target="tpu_custom_call" | custom-call | tf_op jit(solution)/shard_map/write_results/pallas_call | solution.py:414

commit v6 on v2

--- a/solution.py
+++ b/solution.py
@@ -14,6 +14,7 @@
 COLS_COLS = (((1,), (1,)), ((), ()))
 COLS_ROWS = (((1,), (0,)), ((), ()))
 MESH = pl.DeviceIdType.MESH
+PIECES = 4
 
 
 def dot(a, b, dims):
@@ -55,10 +56,10 @@
         c.wait()
 
 
-def kernel(tp, x_hbm, gy_hbm, ug_hbm, uu_hbm, wg_hbm, wu_hbm, wd_hbm, xin_hbm, gamma_ref, gr_hbm, o_hbm, wo_hbm,
+def kernel(tp, x_hbm, gy_hbm, ug_hbm, uu_hbm, wg_hbm, wu_hbm, wd_hbm, xin_hbm, gamma_hbm, gr_hbm, o_hbm, wo_hbm,
            dso, dob, dwgu, dwd, dwo,
-           gy, xb, part, peer, hop, froml, fromr, du, wgu, wd, wo, ugb, uub, ob, xin, gr,
-           s_gy, r_gy, s_x, r_x, s_p, r_p, s_h, r_h, s_t, r_t, s_ds, r_ds,
+           gy, xb, part, peer, hop, froml, fromr, du, wgu, wd, wo, ugb, uub, ob, xin, gr, gamma_ref,
+           s_gy, r_gy, s_x, r_x, s_p, r_p, s_h, r_h, s_t, r_t, s_ds, r_ds, s_e, r_e,
            l_w, l_own, l_u, l_o, l_tok):
     half = gy.shape[1]
     cols = wd.shape[0]
@@ -134,6 +135,7 @@
         c.start()
     pltpu.make_async_copy(xin_hbm, xin, l_tok.at[0]).start()
     pltpu.make_async_copy(gr_hbm, gr, l_tok.at[1]).start()
+    pltpu.make_async_copy(gamma_hbm, gamma_ref, l_tok.at[2]).start()
 
     @pl.loop(0, 32)
     def _(n):
@@ -252,6 +254,7 @@
     ds = gy
     pltpu.make_async_copy(xin_hbm, xin, l_tok.at[0]).wait()
     pltpu.make_async_copy(gr_hbm, gr, l_tok.at[1]).wait()
+    pltpu.make_async_copy(gamma_hbm, gamma_ref, l_tok.at[2]).wait()
     gamma = gamma_ref[...].astype(F32).reshape(1, gamma_ref.shape[0])
 
     def norm_quarter(qi):
@@ -289,46 +292,9 @@
     def _(n):
         o_copy(n).wait()
 
-    @pl.loop(0, 16)
-    def _(u):
-        v, w = u - 4, u - 12
-        i = jnp.where(u < 4, lax.rem(u, 2), jnp.where(u < 12, v // 4, w // 2))
-        k = jnp.where(u < 4, 2 * (u // 2), jnp.where(u < 12, 4 + 2 * lax.rem(v, 4), 12 + 2 * lax.rem(w, 2)))
-
-        @pl.when(k > 0)
-        def _():
-            for d in range(2):
-                n = 2 * (k + d) + i
-                block = q(ds.at[k + d], i)
-                send(block, block, s_ds.at[n], r_ds.at[n], partner).wait_recv()
-
-        @pl.when(k == 4)
-        def _():
-            for src, dst, dev in ((4, 12, right), (5, 13, left)):
-                n = 2 * dst + i
-                send(q(ds.at[src], i), q(ds.at[dst], i), s_ds.at[n], r_ds.at[n], dev).start()
-
-        @pl.when((k > 0) & (lax.rem(k, 4) == 0))
-        def _():
-            for d in range(2):
-                n = 2 * (k + 2 + d) + i
-                send(q(ds.at[k + d], i), q(ds.at[k + 2 + d], i), s_ds.at[n], r_ds.at[n], partner).start()
-
-        rows = pl.ds(pl.multiple_of(i * quarter, quarter), quarter)
-        for d in range(2):
-            block = ds[k + d, rows]
-            n = 2 * (k + d) + i
-            dob[n] = dot(wo[...], block, COLS_COLS).astype(BF16)
-            dwo[...] += dot(ob[n], block, COLS_ROWS)
-
     @pl.loop(2, 16)
     def _(k):
         drain(xb, s_x, k)
-
-    @pl.loop(4, 32)
-    def _(n):
-        block = q(ds.at[n // 2], 0)
-        send(block, block, s_ds.at[n], s_ds.at[n], partner).wait_send()
 
     for j in range(8):
         send(peer.at[j], peer.at[j], s_p.at[j], s_p.at[j], partner).wait_send()
@@ -337,6 +303,74 @@
             hop_copy(12 + side, i).wait_send()
         for qi in range(4):
             tail_copy(side, qi).wait_send()
+
+    def piece_copy(src, dst, e, dev):
+        n = PIECES * (dst - 12) + e
+        rows = pl.ds(quarter + e * (quarter // PIECES), quarter // PIECES)
+        return send(ds.at[src, rows], ds.at[dst, rows], s_e.at[n], r_e.at[n], dev)
+
+    def products(k, i):
+        rows = pl.ds(pl.multiple_of(i * quarter, quarter), quarter)
+        for d in range(2):
+            block = ds[k + d, rows]
+            n = 2 * (k + d) + i
+            dob[n] = dot(wo[...], block, COLS_COLS).astype(BF16)
+            dwo[...] += dot(ob[n], block, COLS_ROWS)
+
+    @pl.loop(0, 14)
+    def _(u):
+        v, w = u - 4, u - 12
+        i = jnp.where(u < 4, lax.rem(u, 2), jnp.where(u < 12, v // 4, w // 2))
+        k = jnp.where(u < 4, 2 * (u // 2), jnp.where(u < 12, 4 + 2 * lax.rem(v, 4), 12 + 2 * lax.rem(w, 2)))
+
+        @pl.when(k > 0)
+        def _():
+            for d in range(2):
+                n = 2 * (k + d) + i
+                block = q(ds.at[k + d], i)
+                send(block, block, s_ds.at[n], r_ds.at[n], partner).wait_recv()
+
+        @pl.when((k == 4) & (i == 0))
+        def _():
+            for src, dst, dev in ((4, 12, right), (5, 13, left)):
+                ds_copy(src, dst, 0, dev).start()
+
+        @pl.when((k == 4) & (i == 1))
+        def _():
+            for e in range(PIECES):
+                for src, dst, dev in ((4, 12, right), (5, 13, left)):
+                    piece_copy(src, dst, e, dev).start()
+
+        @pl.when((k > 0) & (lax.rem(k, 4) == 0))
+        def _():
+            for d in range(2):
+                n = 2 * (k + 2 + d) + i
+                send(q(ds.at[k + d], i), q(ds.at[k + 2 + d], i), s_ds.at[n], r_ds.at[n], partner).start()
+
+        products(k, i)
+
+    for e in range(PIECES):
+        for d in range(2):
+            piece_copy(12 + d, 12 + d, e, partner).wait_recv()
+            piece_copy(12 + d, 14 + d, e, partner).start()
+    products(12, 1)
+    for e in range(PIECES):
+        for d in range(2):
+            piece_copy(14 + d, 14 + d, e, partner).wait_recv()
+    products(14, 1)
+
+    @pl.loop(4, 28)
+    def _(n):
+        @pl.when((n < 24) | (lax.rem(n, 2) == 0))
+        def _():
+            block = q(ds.at[n // 2], 0)
+            send(block, block, s_ds.at[n], s_ds.at[n], partner).wait_send()
+
+    for i in (28, 30):
+        ds_copy(14, i // 2, 0, partner).wait_send()
+    for e in range(PIECES):
+        for dst in range(12, 16):
+            piece_copy(dst, dst, e, partner).wait_send()
 
 
 def solution(mesh):
@@ -364,7 +398,7 @@
                 pltpu.VMEM((cols, hid), F32),
                 pltpu.VMEM((ocols, hid), F32),
             ),
-            in_specs=[any_spec] * 8 + [vmem_spec] + [any_spec] * 3,
+            in_specs=[any_spec] * 12,
             out_specs=(vmem_spec,) * 5,
             scratch_shapes=[
                 pltpu.VMEM((16, half, hid), BF16),
@@ -383,13 +417,15 @@
                 pltpu.VMEM((32, ocols, quarter), BF16),
                 pltpu.VMEM((rows, hid), BF16),
                 pltpu.VMEM((rows, hid), BF16),
+                pltpu.VMEM((hid,), BF16),
                 dma((16,)), dma((16,)),
                 dma((16,)), dma((16,)),
                 dma((8,)), dma((8,)),
                 dma((4,)), dma((4,)),
                 dma((8,)), dma((8,)),
                 dma((32,)), dma((32,)),
-                dma((4,)), dma((4,)), dma((4,)), dma((32,)), dma((2,)),
+                dma((4 * PIECES,)), dma((4 * PIECES,)),
+                dma((4,)), dma((4,)), dma((4,)), dma((32,)), dma((3,)),
             ],
             compiler_params=pltpu.CompilerParams(
                 collective_id=0, has_side_effects=True, vmem_limit_bytes=54_000_000),

time: 133 us -> 132 us (level)
  no operation moved by 1% of the time
where the time goes in v6:
time: 132 us
  Pallas kernels  131 us (99%)
    pallas_call x1, Pallas kernels, local_backward(): pl.pallas_call(functools.partial(kernel, tp), out_shape=(pltpu.VMEM((rows...  128 us
    pallas_call x1, Pallas kernels, local_backward(): pl.pallas_call(functools.partial(write_kernel, tp, half), out_shape=(jax....  3.7 us

profile of v6, /device:TPU:81, one launch (start us, length us, event | category | flops | bytes accessed | tf_op | source)
XLA Modules:
  0.0 132.1 jit_solution(2942568454476518549)
XLA Ops:
  0.6 127.7 %layer_backward.1 = (bf16[512,896]{1,0:T(8,128)(2,1)S(1)}, bf16[32,112,128]{2,1,0:T(8,128)(2,1)S(1)}, f32[1216,896]{1,0:T(8,128)S(1)}, f32[608,896]{1,0:T(8,128)S(1)}, f32[112,896]{1,0:T(8,128)S(1)}) custom-call(bf16[512,896]{1,0:T(8,128)(2,1)} %x_hbm.1, bf16[512,896]{1,0:T(8,128)(2,1)} %gy_hbm.1, bf16[608,4096]{1,0:T(8,128)(2,1)} %bitcast.8, ...), custom_call_target="tpu_custom_call" | custom-call | tf_op jit(solution)/shard_map/layer_backward/pallas_call | solution.py:392
  128.4 3.7 %write_results.1 = (bf16[512,896]{1,0:T(8,128)(2,1)}, bf16[112,4096]{1,0:T(8,128)(2,1)}, f32[608,896]{1,0:T(8,128)}, f32[608,896]{1,0:T(8,128)}, f32[608,896]{1,0:T(8,128)}, /*index=5*/f32[112,896]{1,0:T(8,128)}) custom-call(bf16[512,896]{1,0:T(8,128)(2,1)S(1)} %get-tuple-element.17.dso, bf16[32,112,128]{2,1,0:T(8,128)(2,1)S(1)} %get-tuple-element.18.dob, ...), custom_call_target="tpu_custom_call" | custom-call | tf_op jit(solution)/shard_map/write_results/pallas_call | solution.py:436

commit v7 on v6

v7 whole, which is shorter than its diff:
```python
import functools

import jax
import jax.numpy as jnp
from jax import lax
from jax.experimental import pallas as pl
from jax.experimental.pallas import tpu as pltpu
from jax.sharding import PartitionSpec as P

NORM_EPS = 1e-5
F32 = jnp.float32
BF16 = jnp.bfloat16
ROWS_ROWS = (((0,), (0,)), ((), ()))
COLS_COLS = (((1,), (1,)), ((), ()))
COLS_ROWS = (((1,), (0,)), ((), ()))
MESH = pl.DeviceIdType.MESH
PIECES = 4


def dot(a, b, dims):
    return lax.dot_general(a, b, dims, preferred_element_type=F32)


def slot_token(tp, half, k):
    me = lax.axis_index("tp")
    g, b, i = k // 4, lax.rem(k, 4) // 2, lax.rem(k, 2)
    dx = jnp.where(g == 0, 0, jnp.where(g == 3, 2, 2 * i - 1))
    h = jnp.where(g == 2, 1 - i, i)
    chip = lax.rem(me // 2 + dx + tp // 2, tp // 2)
    shard = 2 * chip + lax.rem(lax.rem(me, 2) + b, 2)
    return pl.multiple_of((2 * shard + h) * half, half)


def write_kernel(dso, dob, dwgu, dwd, dwo, ds_out, do_out, dwg_out, dwu_out, dwd_out, dwo_out, sem):
    cols = dwd.shape[0]
    copies = [pltpu.make_async_copy(src, dst, sem) for src, dst in (
        (dwgu.at[pl.ds(0, cols)], dwg_out), (dwgu.at[pl.ds(cols, cols)], dwu_out), (dwd, dwd_out), (dso, ds_out),
        (dob, do_out), (dwo, dwo_out))]
    for c in copies:
        c.start()
    for c in copies:
        c.wait()


def kernel(tp, x_hbm, gy_hbm, ug_hbm, uu_hbm, wg_hbm, wu_hbm, wd_hbm, xin_hbm, gamma_hbm, gr_hbm, o_hbm, wo_hbm,
           dso, dob, dwgu, dwd, dwo,
           gy, xb, part, peer, hop, frm, du, weights, ub, ob, tok, gamma_ref,
           sent, r_gy, r_x, r_e, r_t, r_p, r_h, l_u, l_w, l_o, l_tok, l_gamma):
    half = gy.shape[1]
    cols, ocols = dwd.shape[0], dwo.shape[0]
    wgu = weights.at[pl.ds(0, 2 * cols)]
    wd = weights.at[pl.ds(2 * cols, cols)]
    wo = weights.at[pl.ds(3 * cols, ocols)]
    s_gy, s_x, s_p, s_h, s_t, s_ds = (sent.at[i] for i in range(6))
    quarter = half // 2
    me = lax.axis_index("tp")
    right = lax.rem(me + 2, tp)
    left = lax.rem(me + tp - 2, tp)
    partner = me + 1 - 2 * lax.rem(me, 2)
    slot_row = functools.partial(slot_token, tp, half)

    def send(src, dst, ssem, rsem, dev):
        return pltpu.make_async_remote_copy(
            src_ref=src, dst_ref=dst, send_sem=ssem, recv_sem=rsem, device_id={"tp": dev}, device_id_type=MESH)

    def u_copies(k):
        tokens = pl.ds(slot_row(k), half)
        at = lax.rem(k, 2)
        return (pltpu.make_async_copy(ug_hbm.at[:, tokens], ub.at[at, 0], l_u.at[at]),
                pltpu.make_async_copy(uu_hbm.at[:, tokens], ub.at[at, 1], l_u.at[at]))

    def o_copy(n):
        tokens = pl.ds(pl.multiple_of(slot_row(n // 2) + lax.rem(n, 2) * quarter, quarter), quarter)
        return pltpu.make_async_copy(o_hbm.at[:, tokens], ob.at[n], l_o)

    def own(hbm, h):
        return hbm.at[pl.ds(h * half, half)]

    barrier = pltpu.get_barrier_semaphore()
    for dev in (left, right, partner):
        pl.semaphore_signal(barrier, inc=1, device_id={"tp": dev}, device_id_type=MESH)
    pl.semaphore_wait(barrier, 3)

    def send_own(hbm, buf, ssem, rsem):
        for src, dst, dev in ((0, 4, right), (1, 5, left), (1, 8, right), (0, 9, left), (0, 2, partner), (1, 3, partner)):
            send(own(hbm, src), buf.at[dst], ssem, rsem.at[dst // 2], dev).start()

    def arrived(ref, rsem):
        pltpu.make_async_copy(ref, ref, rsem).wait()

    def left_here(ref, ssem):
        send(ref, ref, ssem, ssem, partner).wait_send()

    def gather_step(buf, ssem, rsem, k, also):
        place = lax.rem(k, 4)

        @pl.when((k >= 2) & (lax.rem(place, 2) == 0))
        def _():
            arrived(buf.at[pl.ds(k, 2)], rsem.at[k // 2])

        @pl.when(k == 4)
        def _():
            send(buf.at[4], buf.at[12], ssem, rsem.at[6], right).start()
            send(buf.at[5], buf.at[13], ssem, rsem.at[6], left).start()

        @pl.when((k >= 4) & (place == 0))
        def _():
            for d in range(2):
                send(buf.at[k + d], buf.at[k + 2 + d], ssem, rsem.at[k // 2 + 1], partner).start()
            if also is not None:
                pl.when(k == 4)(also)

    send_own(gy_hbm, gy, s_gy, r_gy)
    for h in range(2):
        pltpu.make_async_copy(own(gy_hbm, h), gy.at[h], r_gy.at[0]).start()
        pltpu.make_async_copy(own(x_hbm, h), xb.at[h], r_x.at[0]).start()
    for i, src in enumerate((wg_hbm, wu_hbm, wd_hbm, wo_hbm)):
        pltpu.make_async_copy(src, weights.at[pl.ds(i * cols, src.shape[0])], l_w).start()
    for c in u_copies(0):
        c.start()
    pltpu.make_async_copy(xin_hbm, tok.at[0], l_tok).start()
    pltpu.make_async_copy(gr_hbm, tok.at[1], l_tok).start()
    pltpu.make_async_copy(gamma_hbm, gamma_ref, l_gamma).start()

    @pl.loop(0, 32)
    def _(n):
        o_copy(n).start()

    dwd[...] = jnp.zeros_like(dwd)
    dwgu[...] = jnp.zeros_like(dwgu)
    dwo[...] = jnp.zeros_like(dwo)
    arrived(weights, l_w)
    arrived(gy.at[pl.ds(0, 2)], r_gy.at[0])
    arrived(xb.at[pl.ds(0, 2)], r_x.at[0])

    def part_copy(k):
        j = (k // 4) * 2 + lax.rem(k, 2)
        return send(part.at[k], peer.at[j], s_p, r_p, partner)

    @pl.loop(0, 16)
    def _(k):
        @pl.when(k + 1 < 16)
        def _():
            for c in u_copies(k + 1):
                c.start()

        @pl.when((k > 0) & (lax.rem(k + 3, 4) >= 2))
        def _():
            part_copy(k - 1).start()

        gather_step(gy, s_gy, r_gy, k, lambda: send_own(x_hbm, xb, s_x, r_x))
        at = lax.rem(k, 2)
        arrived(ub.at[at], l_u.at[at])
        gyk = gy[k]
        gh = dot(wd[...], gyk, COLS_COLS)
        gate = ub[at, 0].astype(F32)
        up = ub[at, 1].astype(F32)
        sig = jax.nn.sigmoid(gate)
        act = gate * sig
        silu = sig * (1.0 + gate * (1.0 - sig))
        z = (act * up).astype(BF16)
        du_up = (gh * act).astype(BF16)
        du_gate = (gh * up * silu).astype(BF16)
        du[k, pl.ds(0, cols)] = du_gate
        du[k, pl.ds(cols, cols)] = du_up
        dwd[...] += dot(z, gyk, COLS_ROWS)
        part[k] = dot(du[k], wgu[...], ROWS_ROWS).astype(BF16)

    part_copy(15).start()

    left_here(gy.at[pl.ds(0, 14)], s_gy)

    def add_peer(k, more=()):
        j = (k // 4) * 2 + k % 2
        t = part[k].astype(F32) + peer[j].astype(F32)
        for m in more:
            t = t + m[...].astype(F32)
        part[k] = t.astype(BF16)

    def q(ref, i):
        return ref.at[pl.ds(i * quarter, quarter)]

    arrived(peer, r_p)

    def hop_copy(k, i):
        side = k - 12
        return send(q(part.at[k], i), q(hop.at[side], i), s_h, r_h, (right, left)[side])

    for k in (12, 13):
        add_peer(k)
    for i in range(2):
        for k in (12, 13):
            hop_copy(k, i).start()

    def dw_step(j):
        xk = xb[pl.ds(2 * j, 2)].reshape(2 * half, xb.shape[2])
        duk = jnp.concatenate((du[2 * j], du[2 * j + 1]), axis=1)
        dwgu[...] += dot(duk, xk, COLS_ROWS)

    def tail_copy(side, qi):
        k = ((9, 5), (4, 8))[side][qi // 2]
        return send(q(part.at[k], qi % 2), frm.at[qi, side], s_t, r_t.at[qi], (right, left)[side])

    tail_order = ((2, 0, 3, 1), (0, 2, 1, 3))

    def tails():
        add_peer(5)
        add_peer(4)
        arrived(hop, r_h)
        add_peer(9, (hop.at[0],))
        add_peer(8, (hop.at[1],))
        for n in range(4):
            for side in range(2):
                tail_copy(side, tail_order[side][n]).start()

    @pl.loop(0, 8)
    def _(j):
        pl.when(j == 6)(tails)
        gather_step(xb, s_x, r_x, 2 * j, None)
        dw_step(j)

    ds = gy
    arrived(tok, l_tok)
    arrived(gamma_ref, l_gamma)
    gamma = gamma_ref[...].astype(F32).reshape(1, gamma_ref.shape[0])

    def norm_quarter(qi):
        h, i = qi // 2, qi % 2
        arrived(frm.at[qi], r_t.at[qi])
        step = 32

        @pl.loop(0, quarter // step)
        def _(n):
            rows = pl.ds(pl.multiple_of(n * step, step), step)
            inner = pl.ds(pl.multiple_of(i * quarter + n * step, step), step)
            tokens = pl.ds(pl.multiple_of(qi * quarter + n * step, step), step)
            dx = (part[h, inner].astype(F32) + peer[h, inner].astype(F32)
                  + frm[qi, 0, rows].astype(F32) + frm[qi, 1, rows].astype(F32)).astype(BF16)
            xf = tok[0, tokens].astype(F32)
            inv = lax.rsqrt(jnp.mean(xf * xf, axis=-1, keepdims=True) + NORM_EPS)
            scaled = dx.astype(F32) * gamma
            proj = jnp.mean(scaled * xf, axis=-1, keepdims=True)
            out = (tok[1, tokens].astype(F32) + inv * (scaled - xf * (inv * inv) * proj)).astype(BF16)
            ds[h, inner] = out
            dso[tokens] = out

    def ds_copy(src, dst, i, dev):
        return send(q(ds.at[src], i), q(ds.at[dst], i), s_ds, r_gy.at[dst // 2 + 7 * i], dev)

    for i in range(2):
        for h in (0, 1):
            norm_quarter(2 * h + i)
        for src, dst, dev in ((0, 4, right), (1, 5, left), (1, 8, right), (0, 9, left), (0, 2, partner), (1, 3, partner)):
            ds_copy(src, dst, i, dev).start()

    arrived(ob, l_o)
    left_here(xb.at[pl.ds(0, 14)], s_x)
    left_here(peer, s_p)
    left_here(hop, s_h)
    left_here(frm, s_t)

    def piece_copy(src, dst, e, dev):
        rows = pl.ds(quarter + e * (quarter // PIECES), quarter // PIECES)
        return send(ds.at[src, rows], ds.at[dst, rows], s_ds, r_e.at[PIECES * (dst // 2 - 6) + e], dev)

    def piece_arrived(k, e):
        rows = pl.ds(quarter + e * (quarter // PIECES), quarter // PIECES)
        arrived(ds.at[pl.ds(k, 2), rows], r_e.at[PIECES * (k // 2 - 6) + e])

    def products(k, i):
        rows = pl.ds(pl.multiple_of(i * quarter, quarter), quarter)
        for d in range(2):
            block = ds[k + d, rows]
            n = 2 * (k + d) + i
            tokens = pl.ds(pl.multiple_of(slot_row(k + d) + i * quarter, quarter), quarter)
            dob[:, tokens] = dot(wo[...], block, COLS_COLS).astype(BF16)
            dwo[...] += dot(ob[n], block, COLS_ROWS)

    @pl.loop(0, 14)
    def _(u):
        v, w = u - 4, u - 12
        i = jnp.where(u < 4, lax.rem(u, 2), jnp.where(u < 12, v // 4, w // 2))
        k = jnp.where(u < 4, 2 * (u // 2), jnp.where(u < 12, 4 + 2 * lax.rem(v, 4), 12 + 2 * lax.rem(w, 2)))

        @pl.when(k > 0)
        def _():
            rows = pl.ds(pl.multiple_of(i * quarter, quarter), quarter)
            arrived(ds.at[pl.ds(k, 2), rows], r_gy.at[k // 2 + 7 * i])

        @pl.when((k == 4) & (i == 0))
        def _():
            for src, dst, dev in ((4, 12, right), (5, 13, left)):
                ds_copy(src, dst, 0, dev).start()

        @pl.when((k == 4) & (i == 1))
        def _():
            for e in range(PIECES):
                for src, dst, dev in ((4, 12, right), (5, 13, left)):
                    piece_copy(src, dst, e, dev).start()

        @pl.when((k > 0) & (lax.rem(k, 4) == 0))
        def _():
            for d in range(2):
                ds_copy(k + d, k + 2 + d, i, partner).start()

        products(k, i)

    for e in range(PIECES):
        piece_arrived(12, e)
        for d in range(2):
            piece_copy(12 + d, 14 + d, e, partner).start()
    products(12, 1)
    for e in range(PIECES):
        piece_arrived(14, e)
    products(14, 1)
    left_here(ds.at[pl.ds(0, 14)], s_ds)


def solution(mesh):
    tp = mesh.shape["tp"]
    token_spec = P(("dp", "tp"), None)
    split_cols = P("dp", "tp")
    weight_cols = P(None, "tp")
    weight_rows = P("tp", None)

    def local_backward(x_norm, grad_y, u_gate, u_up, w_gate, w_up, w_down, x_in, gamma, grad_res, attn_out, w_out):
        rows, hid = x_norm.shape
        tokens, cols = u_gate.shape
        ocols = attn_out.shape[1]
        half = rows // 2
        quarter = half // 2
        any_spec = pl.BlockSpec(memory_space=pl.ANY)
        vmem_spec = pl.BlockSpec(memory_space=pltpu.VMEM)
        dma = pltpu.SemaphoreType.DMA
        results = pl.pallas_call(
            functools.partial(kernel, tp),
            out_shape=(
                pltpu.VMEM((rows, hid), BF16),
                pltpu.VMEM((ocols, tokens), BF16),
                pltpu.VMEM((2 * cols, hid), F32),
                pltpu.VMEM((cols, hid), F32),
                pltpu.VMEM((ocols, hid), F32),
            ),
            in_specs=[any_spec] * 12,
            out_specs=(vmem_spec,) * 5,
            scratch_shapes=[
                pltpu.VMEM((16, half, hid), BF16),
                pltpu.VMEM((16, half, hid), BF16),
                pltpu.VMEM((16, half, hid), BF16),
                pltpu.VMEM((8, half, hid), BF16),
                pltpu.VMEM((2, half, hid), BF16),
                pltpu.VMEM((4, 2, quarter, hid), BF16),
                pltpu.VMEM((16, 2 * cols, half), BF16),
                pltpu.VMEM((3 * cols + ocols, hid), BF16),
                pltpu.VMEM((2, 2, cols, half), BF16),
                pltpu.VMEM((32, ocols, quarter), BF16),
                pltpu.VMEM((2, rows, hid), BF16),
                pltpu.VMEM((hid,), BF16),
                dma((6,)),
                dma((13,)), dma((8,)), dma((2 * PIECES,)), dma((4,)), dma, dma, dma((2,)), dma, dma, dma, dma,
            ],
            compiler_params=pltpu.CompilerParams(
                collective_id=0, has_side_effects=True, vmem_limit_bytes=54_000_000),
            name="layer_backward",
        )(x_norm, grad_y, u_gate.T, u_up.T, w_gate.T, w_up.T, w_down, x_in, gamma, grad_res, attn_out.T,
          w_out)
        results = [pltpu.with_memory_space_constraint(r, pltpu.VMEM) for r in results]
        ds, do, dwg, dwu, dwd, dwo = pl.pallas_call(
            write_kernel,
            out_shape=(
                jax.ShapeDtypeStruct((rows, hid), BF16),
                jax.ShapeDtypeStruct((ocols, tokens), BF16),
                jax.ShapeDtypeStruct((cols, hid), F32),
                jax.ShapeDtypeStruct((cols, hid), F32),
                jax.ShapeDtypeStruct((cols, hid), F32),
                jax.ShapeDtypeStruct((ocols, hid), F32),
            ),
            in_specs=[vmem_spec] * 5,
            out_specs=(any_spec,) * 6,
            scratch_shapes=[dma],
            compiler_params=pltpu.CompilerParams(vmem_limit_bytes=1_000_000),
            name="write_results",
        )(*results)
        return ds, do.T, dwg.T, dwu.T, dwd, dwo

    return jax.shard_map(
        local_backward,
        mesh=mesh,
        in_specs=(token_spec, token_spec, split_cols, split_cols, weight_cols, weight_cols, weight_rows,
                  token_spec, P(None), token_spec, split_cols, weight_rows),
        out_specs=(token_spec, split_cols, split_cols, split_cols, token_spec, token_spec),
        check_vma=False,
    )
```

time: 132 us -> 130 us (0.985)
  Pallas kernels: 131 us -> 129 us
    pallas_call x1, Pallas kernels: 128 us -> 126 us  [local_backward(): pl.pallas_call(functools.partial(kernel, tp), out_shape=(pltpu.VMEM((rows...]
where the time goes in v7:
time: 130 us
  Pallas kernels  129 us (99%)
    pallas_call x1, Pallas kernels, local_backward(): pl.pallas_call(functools.partial(kernel, tp), out_shape=(pltpu.VMEM((rows...  126 us
    pallas_call x1, Pallas kernels, local_backward(): pl.pallas_call(write_kernel, out_shape=(jax.ShapeDtypeStruct((rows, hid),...  3.4 us

profile of v7, /device:TPU:81, one launch (start us, length us, event | category | flops | bytes accessed | tf_op | source)
XLA Modules:
  0.0 129.7 jit_solution(8464828581767861492)
XLA Ops:
  0.6 125.7 %layer_backward.1 = (bf16[512,896]{1,0:T(8,128)(2,1)S(1)}, bf16[112,4096]{1,0:T(8,128)(2,1)S(1)}, f32[1216,896]{1,0:T(8,128)S(1)}, f32[608,896]{1,0:T(8,128)S(1)}, f32[112,896]{1,0:T(8,128)S(1)}) custom-call(bf16[512,896]{1,0:T(8,128)(2,1)} %x_hbm.1, bf16[512,896]{1,0:T(8,128)(2,1)} %gy_hbm.1, bf16[608,4096]{1,0:T(8,128)(2,1)} %bitcast.8, ...), custom_call_target="tpu_custom_call" | custom-call | tf_op jit(solution)/shard_map/layer_backward/pallas_call | solution.py:335
  126.3 3.4 %write_results.1 = (bf16[512,896]{1,0:T(8,128)(2,1)}, bf16[112,4096]{1,0:T(8,128)(2,1)}, f32[608,896]{1,0:T(8,128)}, f32[608,896]{1,0:T(8,128)}, f32[608,896]{1,0:T(8,128)}, /*index=5*/f32[112,896]{1,0:T(8,128)}) custom-call(bf16[512,896]{1,0:T(8,128)(2,1)S(1)} %get-tuple-element.17.dso, bf16[112,4096]{1,0:T(8,128)(2,1)S(1)} %get-tuple-element.18.dob, ...), custom_call_target="tpu_custom_call" | custom-call | tf_op jit(solution)/shard_map/write_results/pallas_call | solution.py:368

commit v8 on v7

--- a/solution.py
+++ b/solution.py
@@ -31,27 +31,54 @@
     return pl.multiple_of((2 * shard + h) * half, half)
 
 
-def write_kernel(dso, dob, dwgu, dwd, dwo, ds_out, do_out, dwg_out, dwu_out, dwd_out, dwo_out, sem):
-    cols = dwd.shape[0]
+def write_kernel(tp, half, dso, dob, dwgu, dwd, dwo, late, o_hbm, wo_hbm, ds_out, do_out, dwg_out, dwu_out, dwd_out, dwo_out,
+                 ob, wo, dob_late, dwo_all, l_in, sem):
+    cols, quarter = dwd.shape[0], half // 2
+    first = slot_token(tp, half, 14)
+
+    def tokens(n):
+        return pl.ds(pl.multiple_of(first + n * quarter, quarter), quarter)
+
+    def shard(n):
+        rows = pl.ds(pl.multiple_of(lax.rem(first + n * 2 * half, tp * 2 * half), 2 * half), 2 * half)
+        return dob.at[:, rows], do_out.at[:, rows]
+
+    loads = [pltpu.make_async_copy(wo_hbm, wo, l_in)] + [
+        pltpu.make_async_copy(o_hbm.at[:, tokens(2 * d + 1)], ob.at[d], l_in) for d in range(2)]
+    for c in loads:
+        c.start()
     copies = [pltpu.make_async_copy(src, dst, sem) for src, dst in (
         (dwgu.at[pl.ds(0, cols)], dwg_out), (dwgu.at[pl.ds(cols, cols)], dwu_out), (dwd, dwd_out), (dso, ds_out),
-        (dob, do_out), (dwo, dwo_out))]
+        *(shard(n) for n in range(1, tp)), *((dob.at[:, tokens(n)], do_out.at[:, tokens(n)]) for n in (0, 2)))]
     for c in copies:
         c.start()
-    for c in copies:
+    for c in loads:
         c.wait()
+    total = dwo[...]
+    for d in range(2):
+        dob_late[d] = dot(wo[...], late[d], COLS_COLS).astype(BF16)
+        total = total + dot(ob[d], late[d], COLS_ROWS)
+    dwo_all[...] = total
+    last = [pltpu.make_async_copy(dwo_all, dwo_out, sem)] + [
+        pltpu.make_async_copy(dob_late.at[d], do_out.at[:, tokens(2 * d + 1)], sem) for d in range(2)]
+    for c in last:
+        c.start()
+    for c in copies + last:
+        c.wait()
 
 
 def kernel(tp, x_hbm, gy_hbm, ug_hbm, uu_hbm, wg_hbm, wu_hbm, wd_hbm, xin_hbm, gamma_hbm, gr_hbm, o_hbm, wo_hbm,
-           dso, dob, dwgu, dwd, dwo,
+           dso, dob, dwgu, dwd, dwo, late,
            gy, xb, part, peer, hop, frm, du, weights, ub, ob, tok, gamma_ref,
-           sent, r_gy, r_x, r_e, r_t, r_p, r_h, l_u, l_w, l_o, l_tok, l_gamma):
+           sent, r_gy, r_x, r_e, r_t, r_p, r_h, l_u, l_w):
     half = gy.shape[1]
     cols, ocols = dwd.shape[0], dwo.shape[0]
     wgu = weights.at[pl.ds(0, 2 * cols)]
     wd = weights.at[pl.ds(2 * cols, cols)]
     wo = weights.at[pl.ds(3 * cols, ocols)]
-    s_gy, s_x, s_p, s_h, s_t, s_ds = (sent.at[i] for i in range(6))
+    s_gy, s_x, s_p = (sent.at[i] for i in range(3))
+    s_h = s_t = s_gy
+    s_ds = s_x
     quarter = half // 2
     me = lax.axis_index("tp")
     right = lax.rem(me + 2, tp)
@@ -71,7 +98,7 @@
 
     def o_copy(n):
         tokens = pl.ds(pl.multiple_of(slot_row(n // 2) + lax.rem(n, 2) * quarter, quarter), quarter)
-        return pltpu.make_async_copy(o_hbm.at[:, tokens], ob.at[n], l_o)
+        return pltpu.make_async_copy(o_hbm.at[:, tokens], ob.at[n], l_w)
 
     def own(hbm, h):
         return hbm.at[pl.ds(h * half, half)]
@@ -118,20 +145,20 @@
         pltpu.make_async_copy(src, weights.at[pl.ds(i * cols, src.shape[0])], l_w).start()
     for c in u_copies(0):
         c.start()
-    pltpu.make_async_copy(xin_hbm, tok.at[0], l_tok).start()
-    pltpu.make_async_copy(gr_hbm, tok.at[1], l_tok).start()
-    pltpu.make_async_copy(gamma_hbm, gamma_ref, l_gamma).start()
-
-    @pl.loop(0, 32)
-    def _(n):
-        o_copy(n).start()
-
     dwd[...] = jnp.zeros_like(dwd)
     dwgu[...] = jnp.zeros_like(dwgu)
     dwo[...] = jnp.zeros_like(dwo)
     arrived(weights, l_w)
     arrived(gy.at[pl.ds(0, 2)], r_gy.at[0])
     arrived(xb.at[pl.ds(0, 2)], r_x.at[0])
+
+    pltpu.make_async_copy(xin_hbm, tok.at[0], r_gy.at[0]).start()
+    pltpu.make_async_copy(gr_hbm, tok.at[1], r_gy.at[0]).start()
+    pltpu.make_async_copy(gamma_hbm, gamma_ref, r_x.at[0]).start()
+
+    @pl.loop(0, 32)
+    def _(n):
+        o_copy(n).start()
 
     def part_copy(k):
         j = (k // 4) * 2 + lax.rem(k, 2)
@@ -199,7 +226,7 @@
 
     def tail_copy(side, qi):
         k = ((9, 5), (4, 8))[side][qi // 2]
-        return send(q(part.at[k], qi % 2), frm.at[qi, side], s_t, r_t.at[qi], (right, left)[side])
+        return send(q(part.at[k], qi % 2), frm.at[qi % 2, qi // 2, side], s_t, r_t.at[qi % 2], (right, left)[side])
 
     tail_order = ((2, 0, 3, 1), (0, 2, 1, 3))
 
@@ -220,13 +247,14 @@
         dw_step(j)
 
     ds = gy
-    arrived(tok, l_tok)
-    arrived(gamma_ref, l_gamma)
+    arrived(tok, r_gy.at[0])
+    arrived(gamma_ref, r_x.at[0])
+    left_here(xb.at[pl.ds(0, 14)], s_x)
+    left_here(peer, s_p)
     gamma = gamma_ref[...].astype(F32).reshape(1, gamma_ref.shape[0])
 
     def norm_quarter(qi):
         h, i = qi // 2, qi % 2
-        arrived(frm.at[qi], r_t.at[qi])
         step = 32
 
         @pl.loop(0, quarter // step)
@@ -235,7 +263,7 @@
             inner = pl.ds(pl.multiple_of(i * quarter + n * step, step), step)
             tokens = pl.ds(pl.multiple_of(qi * quarter + n * step, step), step)
             dx = (part[h, inner].astype(F32) + peer[h, inner].astype(F32)
-                  + frm[qi, 0, rows].astype(F32) + frm[qi, 1, rows].astype(F32)).astype(BF16)
+                  + frm[i, h, 0, rows].astype(F32) + frm[i, h, 1, rows].astype(F32)).astype(BF16)
             xf = tok[0, tokens].astype(F32)
             inv = lax.rsqrt(jnp.mean(xf * xf, axis=-1, keepdims=True) + NORM_EPS)
             scaled = dx.astype(F32) * gamma
@@ -248,24 +276,17 @@
         return send(q(ds.at[src], i), q(ds.at[dst], i), s_ds, r_gy.at[dst // 2 + 7 * i], dev)
 
     for i in range(2):
+        arrived(frm.at[i], r_t.at[i])
         for h in (0, 1):
             norm_quarter(2 * h + i)
         for src, dst, dev in ((0, 4, right), (1, 5, left), (1, 8, right), (0, 9, left), (0, 2, partner), (1, 3, partner)):
             ds_copy(src, dst, i, dev).start()
 
-    arrived(ob, l_o)
-    left_here(xb.at[pl.ds(0, 14)], s_x)
-    left_here(peer, s_p)
-    left_here(hop, s_h)
-    left_here(frm, s_t)
-
-    def piece_copy(src, dst, e, dev):
-        rows = pl.ds(quarter + e * (quarter // PIECES), quarter // PIECES)
-        return send(ds.at[src, rows], ds.at[dst, rows], s_ds, r_e.at[PIECES * (dst // 2 - 6) + e], dev)
-
-    def piece_arrived(k, e):
-        rows = pl.ds(quarter + e * (quarter // PIECES), quarter // PIECES)
-        arrived(ds.at[pl.ds(k, 2), rows], r_e.at[PIECES * (k // 2 - 6) + e])
+    arrived(ob, l_w)
+    left_here(part.at[pl.ds(0, 6)], s_t)
+
+    def piece(e):
+        return pl.ds(quarter + e * (quarter // PIECES), quarter // PIECES)
 
     def products(k, i):
         rows = pl.ds(pl.multiple_of(i * quarter, quarter), quarter)
@@ -296,7 +317,7 @@
         def _():
             for e in range(PIECES):
                 for src, dst, dev in ((4, 12, right), (5, 13, left)):
-                    piece_copy(src, dst, e, dev).start()
+                    send(ds.at[src, piece(e)], ds.at[dst, piece(e)], s_ds, r_e.at[e], dev).start()
 
         @pl.when((k > 0) & (lax.rem(k, 4) == 0))
         def _():
@@ -306,14 +327,13 @@
         products(k, i)
 
     for e in range(PIECES):
-        piece_arrived(12, e)
+        arrived(ds.at[pl.ds(12, 2), piece(e)], r_e.at[e])
         for d in range(2):
-            piece_copy(12 + d, 14 + d, e, partner).start()
+            to = late.at[d, pl.ds(e * (quarter // PIECES), quarter // PIECES)]
+            send(ds.at[12 + d, piece(e)], to, s_ds, r_e.at[PIECES], partner).start()
     products(12, 1)
-    for e in range(PIECES):
-        piece_arrived(14, e)
-    products(14, 1)
     left_here(ds.at[pl.ds(0, 14)], s_ds)
+    arrived(late, r_e.at[PIECES])
 
 
 def solution(mesh):
@@ -340,24 +360,25 @@
                 pltpu.VMEM((2 * cols, hid), F32),
                 pltpu.VMEM((cols, hid), F32),
                 pltpu.VMEM((ocols, hid), F32),
+                pltpu.VMEM((2, quarter, hid), BF16),
             ),
             in_specs=[any_spec] * 12,
-            out_specs=(vmem_spec,) * 5,
+            out_specs=(vmem_spec,) * 6,
             scratch_shapes=[
                 pltpu.VMEM((16, half, hid), BF16),
                 pltpu.VMEM((16, half, hid), BF16),
                 pltpu.VMEM((16, half, hid), BF16),
                 pltpu.VMEM((8, half, hid), BF16),
                 pltpu.VMEM((2, half, hid), BF16),
-                pltpu.VMEM((4, 2, quarter, hid), BF16),
+                pltpu.VMEM((2, 2, 2, quarter, hid), BF16),
                 pltpu.VMEM((16, 2 * cols, half), BF16),
                 pltpu.VMEM((3 * cols + ocols, hid), BF16),
                 pltpu.VMEM((2, 2, cols, half), BF16),
                 pltpu.VMEM((32, ocols, quarter), BF16),
                 pltpu.VMEM((2, rows, hid), BF16),
                 pltpu.VMEM((hid,), BF16),
-                dma((6,)),
-                dma((13,)), dma((8,)), dma((2 * PIECES,)), dma((4,)), dma, dma, dma((2,)), dma, dma, dma, dma,
+                dma((3,)),
+                dma((13,)), dma((8,)), dma((PIECES + 1,)), dma((2,)), dma, dma, dma((2,)), dma,
             ],
             compiler_params=pltpu.CompilerParams(
                 collective_id=0, has_side_effects=True, vmem_limit_bytes=54_000_000),
@@ -366,7 +387,7 @@
           w_out)
         results = [pltpu.with_memory_space_constraint(r, pltpu.VMEM) for r in results]
         ds, do, dwg, dwu, dwd, dwo = pl.pallas_call(
-            write_kernel,
+            functools.partial(write_kernel, tp, half),
             out_shape=(
                 jax.ShapeDtypeStruct((rows, hid), BF16),
                 jax.ShapeDtypeStruct((ocols, tokens), BF16),
@@ -375,12 +396,18 @@
                 jax.ShapeDtypeStruct((cols, hid), F32),
                 jax.ShapeDtypeStruct((ocols, hid), F32),
             ),
-            in_specs=[vmem_spec] * 5,
+            in_specs=[vmem_spec] * 6 + [pl.BlockSpec(memory_space=pltpu.HBM)] * 2,
             out_specs=(any_spec,) * 6,
-            scratch_shapes=[dma],
-            compiler_params=pltpu.CompilerParams(vmem_limit_bytes=1_000_000),
+            scratch_shapes=[
+                pltpu.VMEM((2, ocols, quarter), BF16),
+                pltpu.VMEM((ocols, hid), BF16),
+                pltpu.VMEM((2, ocols, quarter), BF16),
+                pltpu.VMEM((ocols, hid), F32),
+                dma, dma,
+            ],
+            compiler_params=pltpu.CompilerParams(vmem_limit_bytes=4_000_000),
             name="write_results",
-        )(*results)
+        )(*results, attn_out.T, w_out)
         return ds, do.T, dwg.T, dwu.T, dwd, dwo
 
     return jax.shard_map(

time: 130 us -> 130 us (level)
  no operation moved by 1% of the time
where the time goes in v8:
time: 130 us
  Pallas kernels  129 us (99%)
    pallas_call x1, Pallas kernels, local_backward(): pl.pallas_call(functools.partial(kernel, tp), out_shape=(pltpu.VMEM((rows...  125 us
    pallas_call x1, Pallas kernels, local_backward(): pl.pallas_call(functools.partial(write_kernel, tp, half), out_shape=(jax....  3.68 us

profile of v8, /device:TPU:81, one launch (start us, length us, event | category | flops | bytes accessed | tf_op | source)
XLA Modules:
  0.0 129.5 jit_solution(1481340280237740577)
XLA Ops:
  0.6 0.0 copy-start
  0.6 0.0 copy-start.1
  0.7 125.2 %layer_backward.1 = (bf16[512,896]{1,0:T(8,128)(2,1)S(1)}, bf16[112,4096]{1,0:T(8,128)(2,1)S(1)}, f32[1216,896]{1,0:T(8,128)S(1)}, f32[608,896]{1,0:T(8,128)S(1)...) custom-call(bf16[512,896]{1,0:T(8,128)(2,1)} %x_hbm.1, bf16[512,896]{1,0:T(8,128)(2,1)} %gy_hbm.1, ...), custom_call_target="tpu_custom_call" | custom-call | tf_op jit(solution)/shard_map/layer_backward/pallas_call | solution.py:355
  125.8 0.0 copy-done
  125.8 0.0 copy-done.1
  125.8 3.7 %write_results.1 = (bf16[512,896]{1,0:T(8,128)(2,1)}, bf16[112,4096]{1,0:T(8,128)(2,1)}, f32[608,896]{1,0:T(8,128)}, f32[608,896]{1,0:T(8,128)}, f32[608,896]{1,0:T(8,128)}, /*index=5*/f32[112,896]{1,0:T(8,128)}) custom-call(bf16[512,896]{1,0:T(8,128)(2,1)S(1)} %get-tuple-element.18.dso, bf16[112,4096]{1,0:T(8,128)(2,1)S(1)} %get-tuple-element.19.dob, ...), custom_call_target="tpu_custom_call" | custom-call | tf_op jit(solution)/shard_map/write_results/pallas_call | solution.py:389
Async XLA Ops:
  0.6 125.2 %copy-start = (bf16[4096,112]{0,1:T(8,128)(2,1)S(1)}, bf16[4096,112]{0,1:T(8,128)(2,1)}, u32[]{:S(2)}) copy-start(bf16[4096,112]{0,1:T(8,128)(2,1)} %param.22) | copy-start | bytes 2752516
  0.6 125.2 %copy-start.1 = (bf16[112,896]{1,0:T(8,128)(2,1)S(1)}, bf16[112,896]{1,0:T(8,128)(2,1)}, u32[]{:S(2)}) copy-start(bf16[112,896]{1,0:T(8,128)(2,1)} %wo_hbm.3) | copy-start | bytes 602116

commit v9 on v8

--- a/solution.py
+++ b/solution.py
@@ -31,8 +31,8 @@
     return pl.multiple_of((2 * shard + h) * half, half)
 
 
-def write_kernel(tp, half, dso, dob, dwgu, dwd, dwo, late, o_hbm, wo_hbm, ds_out, do_out, dwg_out, dwu_out, dwd_out, dwo_out,
-                 ob, wo, dob_late, dwo_all, l_in, sem):
+def write_kernel(tp, half, dso, dob, dwgu, dwd, dwo, late, ob, wo, ds_out, do_out, dwg_out, dwu_out, dwd_out, dwo_out,
+                 dob_late, dwo_all, sem):
     cols, quarter = dwd.shape[0], half // 2
     first = slot_token(tp, half, 14)
 
@@ -43,21 +43,15 @@
         rows = pl.ds(pl.multiple_of(lax.rem(first + n * 2 * half, tp * 2 * half), 2 * half), 2 * half)
         return dob.at[:, rows], do_out.at[:, rows]
 
-    loads = [pltpu.make_async_copy(wo_hbm, wo, l_in)] + [
-        pltpu.make_async_copy(o_hbm.at[:, tokens(2 * d + 1)], ob.at[d], l_in) for d in range(2)]
-    for c in loads:
-        c.start()
     copies = [pltpu.make_async_copy(src, dst, sem) for src, dst in (
         (dwgu.at[pl.ds(0, cols)], dwg_out), (dwgu.at[pl.ds(cols, cols)], dwu_out), (dwd, dwd_out), (dso, ds_out),
         *(shard(n) for n in range(1, tp)), *((dob.at[:, tokens(n)], do_out.at[:, tokens(n)]) for n in (0, 2)))]
     for c in copies:
         c.start()
-    for c in loads:
-        c.wait()
     total = dwo[...]
     for d in range(2):
         dob_late[d] = dot(wo[...], late[d], COLS_COLS).astype(BF16)
-        total = total + dot(ob[d], late[d], COLS_ROWS)
+        total = total + dot(ob[:, tokens(2 * d + 1)], late[d], COLS_ROWS)
     dwo_all[...] = total
     last = [pltpu.make_async_copy(dwo_all, dwo_out, sem)] + [
         pltpu.make_async_copy(dob_late.at[d], do_out.at[:, tokens(2 * d + 1)], sem) for d in range(2)]
@@ -385,7 +379,7 @@
             name="layer_backward",
         )(x_norm, grad_y, u_gate.T, u_up.T, w_gate.T, w_up.T, w_down, x_in, gamma, grad_res, attn_out.T,
           w_out)
-        results = [pltpu.with_memory_space_constraint(r, pltpu.VMEM) for r in results]
+        results = [pltpu.with_memory_space_constraint(r, pltpu.VMEM) for r in (*results, attn_out.T, w_out)]
         ds, do, dwg, dwu, dwd, dwo = pl.pallas_call(
             functools.partial(write_kernel, tp, half),
             out_shape=(
@@ -396,18 +390,16 @@
                 jax.ShapeDtypeStruct((cols, hid), F32),
                 jax.ShapeDtypeStruct((ocols, hid), F32),
             ),
-            in_specs=[vmem_spec] * 6 + [pl.BlockSpec(memory_space=pltpu.HBM)] * 2,
+            in_specs=[vmem_spec] * 8,
             out_specs=(any_spec,) * 6,
             scratch_shapes=[
                 pltpu.VMEM((2, ocols, quarter), BF16),
-                pltpu.VMEM((ocols, hid), BF16),
-                pltpu.VMEM((2, ocols, quarter), BF16),
                 pltpu.VMEM((ocols, hid), F32),
-                dma, dma,
+                dma,
             ],
             compiler_params=pltpu.CompilerParams(vmem_limit_bytes=4_000_000),
             name="write_results",
-        )(*results, attn_out.T, w_out)
+        )(*results)
         return ds, do.T, dwg.T, dwu.T, dwd, dwo
 
     return jax.shard_map(

time: 130 us -> 129 us (level)
  no operation moved by 1% of the time
where the time goes in v9:
time: 129 us
  Pallas kernels  129 us (100%)
    pallas_call x1, Pallas kernels, local_backward(): pl.pallas_call(functools.partial(kernel, tp), out_shape=(pltpu.VMEM((rows...  125 us
    pallas_call x1, Pallas kernels, local_backward(): pl.pallas_call(functools.partial(write_kernel, tp, half), out_shape=(jax....  3.41 us

profile of v9, /device:TPU:81, one launch (start us, length us, event | category | flops | bytes accessed | tf_op | source)
XLA Modules:
  0.0 129.3 jit_solution(17089172869316506958)
XLA Ops:
  0.6 0.0 copy-start
  0.6 0.0 copy-start.1
  0.7 125.2 %layer_backward.1 = (bf16[512,896]{1,0:T(8,128)(2,1)S(1)}, bf16[112,4096]{1,0:T(8,128)(2,1)S(1)}, f32[1216,896]{1,0:T(8,128)S(1)}, f32[608,896]{1,0:T(8,128)S(1)...) custom-call(bf16[512,896]{1,0:T(8,128)(2,1)} %x_hbm.1, bf16[512,896]{1,0:T(8,128)(2,1)} %gy_hbm.1, ...), custom_call_target="tpu_custom_call" | custom-call | tf_op jit(solution)/shard_map/layer_backward/pallas_call | solution.py:349
  125.8 0.0 copy-done
  125.8 0.0 copy-done.1
  125.8 3.4 %write_results.1 = (bf16[512,896]{1,0:T(8,128)(2,1)}, bf16[112,4096]{1,0:T(8,128)(2,1)}, f32[608,896]{1,0:T(8,128)}, f32[608,896]{1,0:T(8,128)}, f32[608,896]{1,0:T(8,128)}, /*index=5*/f32[112,896]{1,0:T(8,128)}) custom-call(bf16[512,896]{1,0:T(8,128)(2,1)S(1)} %get-tuple-element.18.dso, bf16[112,4096]{1,0:T(8,128)(2,1)S(1)} %get-tuple-element.19.dob, ...), custom_call_target="tpu_custom_call" | custom-call | tf_op jit(solution)/shard_map/write_results/pallas_call | solution.py:383
Async XLA Ops:
  0.6 125.2 %copy-start = (bf16[4096,112]{0,1:T(8,128)(2,1)S(1)}, bf16[4096,112]{0,1:T(8,128)(2,1)}, u32[]{:S(2)}) copy-start(bf16[4096,112]{0,1:T(8,128)(2,1)} %param.22) | copy-start | bytes 2752516
  0.6 125.2 %copy-start.1 = (bf16[112,896]{1,0:T(8,128)(2,1)S(1)}, bf16[112,896]{1,0:T(8,128)(2,1)}, u32[]{:S(2)}) copy-start(bf16[112,896]{1,0:T(8,128)(2,1)} %wo.1) | copy-start | bytes 602116

commit v10 on v9

--- a/solution.py
+++ b/solution.py
@@ -14,7 +14,7 @@
 COLS_COLS = (((1,), (1,)), ((), ()))
 COLS_ROWS = (((1,), (0,)), ((), ()))
 MESH = pl.DeviceIdType.MESH
-PIECES = 4
+LAST = 16
 
 
 def dot(a, b, dims):
@@ -44,8 +44,9 @@
         return dob.at[:, rows], do_out.at[:, rows]
 
     copies = [pltpu.make_async_copy(src, dst, sem) for src, dst in (
-        (dwgu.at[pl.ds(0, cols)], dwg_out), (dwgu.at[pl.ds(cols, cols)], dwu_out), (dwd, dwd_out), (dso, ds_out),
-        *(shard(n) for n in range(1, tp)), *((dob.at[:, tokens(n)], do_out.at[:, tokens(n)]) for n in (0, 2)))]
+        *((src.at[pl.ds(at + r, cols // 4)], dst.at[pl.ds(r, cols // 4)])
+          for src, at, dst in ((dwgu, 0, dwg_out), (dwgu, cols, dwu_out), (dwd, 0, dwd_out)) for r in range(0, cols, cols // 4)),
+        (dso, ds_out), *(shard(n) for n in range(1, tp)), *((dob.at[:, tokens(n)], do_out.at[:, tokens(n)]) for n in (0, 2)))]
     for c in copies:
         c.start()
     total = dwo[...]
@@ -64,7 +65,7 @@
 def kernel(tp, x_hbm, gy_hbm, ug_hbm, uu_hbm, wg_hbm, wu_hbm, wd_hbm, xin_hbm, gamma_hbm, gr_hbm, o_hbm, wo_hbm,
            dso, dob, dwgu, dwd, dwo, late,
            gy, xb, part, peer, hop, frm, du, weights, ub, ob, tok, gamma_ref,
-           sent, r_gy, r_x, r_e, r_t, r_p, r_h, l_u, l_w):
+           sent, r_gy, r_x, r_t, r_p, r_h, l_u, l_w):
     half = gy.shape[1]
     cols, ocols = dwd.shape[0], dwo.shape[0]
     wgu = weights.at[pl.ds(0, 2 * cols)]
@@ -203,15 +204,10 @@
 
     arrived(peer, r_p)
 
-    def hop_copy(k, i):
-        side = k - 12
-        return send(q(part.at[k], i), q(hop.at[side], i), s_h, r_h, (right, left)[side])
-
     for k in (12, 13):
         add_peer(k)
-    for i in range(2):
-        for k in (12, 13):
-            hop_copy(k, i).start()
+    for side, dev in enumerate((right, left)):
+        send(part.at[12 + side], hop.at[side], s_h, r_h, dev).start()
 
     def dw_step(j):
         xk = xb[pl.ds(2 * j, 2)].reshape(2 * half, xb.shape[2])
@@ -279,8 +275,8 @@
     arrived(ob, l_w)
     left_here(part.at[pl.ds(0, 6)], s_t)
 
-    def piece(e):
-        return pl.ds(quarter + e * (quarter // PIECES), quarter // PIECES)
+    pieces = ((0, quarter - LAST), (quarter - LAST, LAST))
+    r_e, r_late = (r_x.at[1], r_x.at[2]), r_x.at[3]
 
     def products(k, i):
         rows = pl.ds(pl.multiple_of(i * quarter, quarter), quarter)
@@ -309,9 +305,10 @@
 
         @pl.when((k == 4) & (i == 1))
         def _():
-            for e in range(PIECES):
+            for (lo, n), rsem in zip(pieces, r_e):
+                rows = pl.ds(quarter + lo, n)
                 for src, dst, dev in ((4, 12, right), (5, 13, left)):
-                    send(ds.at[src, piece(e)], ds.at[dst, piece(e)], s_ds, r_e.at[e], dev).start()
+                    send(ds.at[src, rows], ds.at[dst, rows], s_ds, rsem, dev).start()
 
         @pl.when((k > 0) & (lax.rem(k, 4) == 0))
         def _():
@@ -320,14 +317,14 @@
 
         products(k, i)
 
-    for e in range(PIECES):
-        arrived(ds.at[pl.ds(12, 2), piece(e)], r_e.at[e])
+    for (lo, n), rsem in zip(pieces, r_e):
+        rows = pl.ds(quarter + lo, n)
+        arrived(ds.at[pl.ds(12, 2), rows], rsem)
         for d in range(2):
-            to = late.at[d, pl.ds(e * (quarter // PIECES), quarter // PIECES)]
-            send(ds.at[12 + d, piece(e)], to, s_ds, r_e.at[PIECES], partner).start()
+            send(ds.at[12 + d, rows], late.at[d, pl.ds(lo, n)], s_ds, r_late, partner).start()
     products(12, 1)
     left_here(ds.at[pl.ds(0, 14)], s_ds)
-    arrived(late, r_e.at[PIECES])
+    arrived(late, r_late)
 
 
 def solution(mesh):
@@ -372,7 +369,7 @@
                 pltpu.VMEM((2, rows, hid), BF16),
                 pltpu.VMEM((hid,), BF16),
                 dma((3,)),
-                dma((13,)), dma((8,)), dma((PIECES + 1,)), dma((2,)), dma, dma, dma((2,)), dma,
+                dma((13,)), dma((8,)), dma((2,)), dma, dma, dma((2,)), dma,
             ],
             compiler_params=pltpu.CompilerParams(
                 collective_id=0, has_side_effects=True, vmem_limit_bytes=54_000_000),

time: 129 us -> 129 us (level)
  no operation moved by 1% of the time
where the time goes in v10:
time: 129 us
  Pallas kernels  129 us (100%)
    pallas_call x1, Pallas kernels, local_backward(): pl.pallas_call(functools.partial(kernel, tp), out_shape=(pltpu.VMEM((rows...  125 us
    pallas_call x1, Pallas kernels, local_backward(): pl.pallas_call(functools.partial(write_kernel, tp, half), out_shape=(jax....  3.4 us

profile of v10, /device:TPU:81, one launch (start us, length us, event | category | flops | bytes accessed | tf_op | source)
XLA Modules:
  0.0 129.4 jit_solution(12622227522200461572)
XLA Ops:
  0.6 0.0 copy-start
  0.6 0.0 copy-start.1
  0.7 125.3 %layer_backward.1 = (bf16[512,896]{1,0:T(8,128)(2,1)S(1)}, bf16[112,4096]{1,0:T(8,128)(2,1)S(1)}, f32[1216,896]{1,0:T(8,128)S(1)}, f32[608,896]{1,0:T(8,128)S(1)...) custom-call(bf16[512,896]{1,0:T(8,128)(2,1)} %x_hbm.1, bf16[512,896]{1,0:T(8,128)(2,1)} %gy_hbm.1, ...), custom_call_target="tpu_custom_call" | custom-call | tf_op jit(solution)/shard_map/layer_backward/pallas_call | solution.py:346
  126.0 0.0 copy-done
  126.0 0.0 copy-done.1
  126.0 3.4 %write_results.1 = (bf16[512,896]{1,0:T(8,128)(2,1)}, bf16[112,4096]{1,0:T(8,128)(2,1)}, f32[608,896]{1,0:T(8,128)}, f32[608,896]{1,0:T(8,128)}, f32[608,896]{1,0:T(8,128)}, /*index=5*/f32[112,896]{1,0:T(8,128)}) custom-call(bf16[512,896]{1,0:T(8,128)(2,1)S(1)} %get-tuple-element.18.dso, bf16[112,4096]{1,0:T(8,128)(2,1)S(1)} %get-tuple-element.19.dob, ...), custom_call_target="tpu_custom_call" | custom-call | tf_op jit(solution)/shard_map/write_results/pallas_call | solution.py:380
Async XLA Ops:
  0.6 125.3 %copy-start = (bf16[4096,112]{0,1:T(8,128)(2,1)S(1)}, bf16[4096,112]{0,1:T(8,128)(2,1)}, u32[]{:S(2)}) copy-start(bf16[4096,112]{0,1:T(8,128)(2,1)} %param.22) | copy-start | bytes 2752516
  0.6 125.3 %copy-start.1 = (bf16[112,896]{1,0:T(8,128)(2,1)S(1)}, bf16[112,896]{1,0:T(8,128)(2,1)}, u32[]{:S(2)}) copy-start(bf16[112,896]{1,0:T(8,128)(2,1)} %wo.1) | copy-start | bytes 602116

commit v11 on v10

--- a/solution.py
+++ b/solution.py
@@ -14,7 +14,6 @@
 COLS_COLS = (((1,), (1,)), ((), ()))
 COLS_ROWS = (((1,), (0,)), ((), ()))
 MESH = pl.DeviceIdType.MESH
-LAST = 16
 
 
 def dot(a, b, dims):
@@ -275,8 +274,8 @@
     arrived(ob, l_w)
     left_here(part.at[pl.ds(0, 6)], s_t)
 
-    pieces = ((0, quarter - LAST), (quarter - LAST, LAST))
-    r_e, r_late = (r_x.at[1], r_x.at[2]), r_x.at[3]
+    pieces = [(quarter * lo // 8, quarter * n // 8) for lo, n in ((0, 4), (4, 2), (6, 1), (7, 1))]
+    r_e, r_late = [r_x.at[1 + e] for e in range(len(pieces))], r_x.at[5]
 
     def products(k, i):
         rows = pl.ds(pl.multiple_of(i * quarter, quarter), quarter)

time: 129 us -> 129 us (level)
  no operation moved by 1% of the time
where the time goes in v11:
time: 129 us
  Pallas kernels  128 us (99%)
    pallas_call x1, Pallas kernels, local_backward(): pl.pallas_call(functools.partial(kernel, tp), out_shape=(pltpu.VMEM((rows...  125 us
    pallas_call x1, Pallas kernels, local_backward(): pl.pallas_call(functools.partial(write_kernel, tp, half), out_shape=(jax....  3.4 us

profile of v11, /device:TPU:81, one launch (start us, length us, event | category | flops | bytes accessed | tf_op | source)
XLA Modules:
  0.0 129.1 jit_solution(9642298735882116130)
XLA Ops:
  0.6 0.0 copy-start
  0.6 0.0 copy-start.1
  0.7 125.0 %layer_backward.1 = (bf16[512,896]{1,0:T(8,128)(2,1)S(1)}, bf16[112,4096]{1,0:T(8,128)(2,1)S(1)}, f32[1216,896]{1,0:T(8,128)S(1)}, f32[608,896]{1,0:T(8,128)S(1)...) custom-call(bf16[512,896]{1,0:T(8,128)(2,1)} %x_hbm.1, bf16[512,896]{1,0:T(8,128)(2,1)} %gy_hbm.1, ...), custom_call_target="tpu_custom_call" | custom-call | tf_op jit(solution)/shard_map/layer_backward/pallas_call | solution.py:345
  125.7 0.0 copy-done
  125.7 0.0 copy-done.1
  125.7 3.4 %write_results.1 = (bf16[512,896]{1,0:T(8,128)(2,1)}, bf16[112,4096]{1,0:T(8,128)(2,1)}, f32[608,896]{1,0:T(8,128)}, f32[608,896]{1,0:T(8,128)}, f32[608,896]{1,0:T(8,128)}, /*index=5*/f32[112,896]{1,0:T(8,128)}) custom-call(bf16[512,896]{1,0:T(8,128)(2,1)S(1)} %get-tuple-element.18.dso, bf16[112,4096]{1,0:T(8,128)(2,1)S(1)} %get-tuple-element.19.dob, ...), custom_call_target="tpu_custom_call" | custom-call | tf_op jit(solution)/shard_map/write_results/pallas_call | solution.py:379
Async XLA Ops:
  0.6 125.1 %copy-start = (bf16[4096,112]{0,1:T(8,128)(2,1)S(1)}, bf16[4096,112]{0,1:T(8,128)(2,1)}, u32[]{:S(2)}) copy-start(bf16[4096,112]{0,1:T(8,128)(2,1)} %param.22) | copy-start | bytes 2752516
  0.6 125.1 %copy-start.1 = (bf16[112,896]{1,0:T(8,128)(2,1)S(1)}, bf16[112,896]{1,0:T(8,128)(2,1)}, u32[]{:S(2)}) copy-start(bf16[112,896]{1,0:T(8,128)(2,1)} %wo.1) | copy-start | bytes 602116
